TPU v7x, 32 devices: a whole 2x2x4 slice. The times are simulated.
32 devices in a mesh: lat: 8 (over z, core), wave: 4 (over y, x).
Axes of the slice: x: 2, y: 2, z: 4, core: 2. Of those that a mesh axis runs over, the one named last changes fastest.
Arguments:
- spectra: bfloat16 [3, 2, 2, 768, 768], P(None, None, None, 'wave', 'lat'), may hold values from -0.01171875 to 0.01171875
- legendre: bfloat16 [16, 768, 768], P('lat', 'wave'), may hold values from -4 to 4
- wave_m: int32 [768], replicated, may hold values from 0 to 767, each once
- nlon: int32 [16], P('lat'), may hold values from 20 to 3088, as said below
- coriolis: float32 [16], P('lat'), may hold values from -1.5 to 1.5
- gauss_quadrature_weight: float32 [16], P('lat'), may hold values from 0.5 to 5
Outputs:
- tendency: float32 [2, 2, 2, 768, 768], P(None, None, None, 'wave', 'lat')
Inputs may be any that keep to these rules, and one draw needn't show every extreme that they name: `nlon`: each value is 20 + 4 i for a whole number i, and some latitude has 3088. `wave_m`: every wavenumber 0 to 767 stands in exactly one slot.
All inputs are finite; a program needn't handle non-finite values.
Results may differ from a plain program's by a relative error of at most 0.0065.
Values may be sent and summed in bfloat16 or wider, within the bound.
No kernel may reach another device: no remote copies, remote signals or barrier semaphores. Data moves between devices by JAX's collectives and lax.ppermute only.
A program may use at most 64 MiB of HBM per device.

v0:
```python
import jax
import jax.numpy as jnp
from jax import lax
from jax.sharding import PartitionSpec as P

NLON = 3088


lon_block = 512
two_pi = 6.283185307179586


def block_count():
    return (NLON + lon_block - 1) // lon_block


def pick_entry(values, position):
    positions = jnp.arange(values.shape[0], dtype=jnp.int32)
    return jnp.sum(jnp.where(positions == position, values, jnp.zeros_like(values)))


def column_factor(wave_ids, count):
    doubled = jnp.where(wave_ids == 0, jnp.float32(1.0), jnp.float32(2.0))
    return jnp.where(2 * wave_ids < count, doubled, jnp.float32(0.0))


def phase_table(wave_ids, first_place, count):
    places = first_place + jnp.arange(lon_block, dtype=jnp.int32)
    residue = places[:, None] * wave_ids[None, :] % count
    angles = two_pi * residue.astype(jnp.float32) / count.astype(jnp.float32)
    return jnp.concatenate([jnp.cos(angles), jnp.sin(angles)], axis=1).astype(jnp.bfloat16)


def inverse_stack(coefficient, multiplier):
    real_part = coefficient[..., 0, :].astype(jnp.float32) * multiplier
    imag_part = -coefficient[..., 1, :].astype(jnp.float32) * multiplier
    return jnp.concatenate([real_part, imag_part], axis=-1).astype(jnp.bfloat16)


def nonlinear(nodal_samples, rotation, places, count):
    vorticity = nodal_samples[..., 0, :]
    velocity_spread_map = nodal_samples[..., 1, :]
    thermal_state_map = nodal_samples[..., 2, :]
    stretch = -(vorticity + rotation) * velocity_spread_map
    thermal_forcing = -thermal_state_map * velocity_spread_map
    paired = jnp.stack([stretch, thermal_forcing], axis=-2)
    return jnp.where(places < count, paired, jnp.zeros_like(paired)).astype(jnp.bfloat16)


def finish(summed_spectra, multiplier, count, weight):
    halfway = summed_spectra.shape[-1] // 2
    scaling_factor = weight / count.astype(jnp.float32)
    real_part = summed_spectra[..., :halfway] * scaling_factor
    imag_part = -summed_spectra[..., halfway:] * scaling_factor
    paired = jnp.stack([real_part, imag_part], axis=-2)
    return jnp.where(multiplier > 0, paired, jnp.zeros_like(paired)).astype(jnp.bfloat16)


def grid_row(piled_arrays, wave_ids, count, rotation, weight, multiplier):

    def one_block(running, block_index):
        first_place = block_index * lon_block
        phases = phase_table(wave_ids, first_place, count)
        nodal_samples = lax.dot_general(
            piled_arrays, phases, (((1,), (1,)), ((), ())), preferred_element_type=jnp.float32
        )
        nodal_samples = nodal_samples.reshape(-1, 3, lon_block)
        places = first_place + jnp.arange(lon_block, dtype=jnp.int32)
        products = nonlinear(nodal_samples, rotation, places, count).reshape(-1, lon_block)
        return (running + jnp.dot(products, phases, preferred_element_type=jnp.float32), None)

    zero_sums = jnp.zeros((piled_arrays.shape[0] // 3 * 2, piled_arrays.shape[1]), jnp.float32)
    summed_spectra, unused = lax.scan(
        one_block, zero_sums, jnp.arange(block_count(), dtype=jnp.int32)
    )
    return finish(summed_spectra.reshape(-1, 2, piled_arrays.shape[1]), multiplier, count, weight)


def local(spectra, legendre, wave_m, nlon, coriolis, gauss_quadrature_weight):
    band_lats, slot_count, wave_total = legendre.shape
    lev_count = spectra.shape[1]
    band_rows = band_lats * lev_count
    wave_rank = lax.axis_index("wave")
    local_ids = lax.dynamic_slice_in_dim(wave_m, wave_rank * slot_count, slot_count, 0)
    totals = jnp.arange(wave_total, dtype=jnp.int32)
    masked = jnp.where(
        totals[None, None, :] >= local_ids[None, :, None], legendre, jnp.zeros_like(legendre)
    )

    def row_facts(row_number):
        latitude_row = row_number // lev_count
        return (
            pick_entry(nlon, latitude_row),
            pick_entry(coriolis, latitude_row),
            pick_entry(gauss_quadrature_weight, latitude_row),
        )

    band_part = masked
    fourier = jnp.einsum(
        "lsn,fvpsn->lvfps",
        band_part,
        lax.all_gather(spectra, "lat", axis=4, tiled=True),
        preferred_element_type=jnp.float32,
    ).astype(jnp.bfloat16)
    fourier = fourier.reshape(band_rows, 3, 2, slot_count)
    gathered = lax.all_to_all(fourier, "wave", split_axis=0, concat_axis=3, tiled=True)
    owned_latitude_rows = gathered.shape[0]

    def full_row(inputs):
        coefficient, offset = inputs
        count, rotation, weight = row_facts(wave_rank * owned_latitude_rows + offset)
        multiplier = column_factor(wave_m, count)
        piled_arrays = inverse_stack(coefficient, multiplier)
        return grid_row(piled_arrays, wave_m, count, rotation, weight, multiplier)[0]

    local_rows = lax.map(full_row, (gathered, jnp.arange(owned_latitude_rows, dtype=jnp.int32)))
    returned = lax.all_to_all(local_rows, "wave", split_axis=3, concat_axis=0, tiled=True)
    returned = returned.reshape(band_lats, lev_count, 2, 2, slot_count)
    turned = lax.all_to_all(masked, "lat", split_axis=2, concat_axis=0, tiled=True)
    band_part = turned
    return jnp.einsum(
        "lsn,lvqps->qvpsn",
        band_part,
        lax.all_gather(returned, "lat", axis=0, tiled=True),
        preferred_element_type=jnp.float32,
    )


def solution(mesh):
    placed = (
        P(None, None, None, "wave", "lat"),
        P("lat", "wave", None),
        P(),
        P("lat"),
        P("lat"),
        P("lat"),
    )
    return jax.shard_map(
        local,
        mesh=mesh,
        in_specs=placed,
        out_specs=P(None, None, None, "wave", "lat"),
        check_vma=False,
    )
```

profile of v0, /device:TPU:0, one launch (start us, length us, event | category | flops | bytes accessed | tf_op | source)
XLA Modules:
  0.0 325.8 jit_solution(5381453114664748880)
XLA Ops:
  6.5 2.2 copy.49
  8.7 0.6 copy.48
  9.6 1.3 fusion.32
  11.0 1.5 copy.61
  12.5 0.6 select_reduce_fusion.2
  13.1 0.6 broadcast_compare_fusion.1
  13.8 2.2 broadcast_select_fusion
  16.0 47.0 %all-gather.2.cloned.1.call-done = bf16[3,2,2,192,768]{3,2,1,0,4:T(2,128)(2,1)} async-done(((bf16[3,2,2,192,96]{3,2,1,0,4:T(2,128)(2,1)}), bf16[3,2,2,192,768]{3,2,1,0,4:T(2,128)(2,1)}) %all-gather.2.cloned.1.call-update) | async-done | bytes 3538960 | tf_op jit(solution)/shard_map/all_gather | solution.py:102
  62.9 16.6 %copy.51 = bf16[3,2,2,192,768]{4,0,2,1,3:T(4,128)(2,1)} copy(bf16[3,2,2,192,768]{3,2,1,0,4:T(2,128)(2,1)} %all-gather.2.cloned.1.call-done) | data formatting | bytes 7077888 | tf_op jit(solution)/shard_map/all_gather | solution.py:102
  79.6 23.1 %fusion.19 = bf16[2,2,3,2,192]{2,0,3,1,4:T(2,128)(2,1)S(1)} fusion(bf16[2,192,768,1,1]{2,0,4,3,1:T(2,128)(2,1)S(1)} %copy.61, bf16[3,2,2,192,768]{4,0,2,1,3:T(4,128)(2,1)} %copy.51), kind=kOutput, calls=%fused_computation.33 | convolution fusion | flops 7082496 | bytes 4137984 | tf_op jit(solution)/shard_map/lsn,fvpsn->lvfps/dot_general | solution.py:99
  102.7 1.1 copy.52
  103.8 3.6 %all-to-all-start = ((bf16[4,3,2,192]{3,2,1,0:T(2,128)(2,1)}), bf16[4,3,2,192]{3,2,1,0:T(2,128)(2,1)S(1)}, u32[]{:S(2)}, u32[]{:S(2)}) async-start(bf16[4,3,2,192]{3,2,1,0:T(2,128)(2,1)} %bitcast.2), calls=%async_computation | async-start | bytes 24576 | tf_op jit(solution)/shard_map/all_to_all | solution.py:106
  107.4 0.7 select_reduce_fusion
  110.7 1.5 all-to-all-done
  112.1 3.5 %all-to-all-start.2 = ((bf16[2,192,768]{1,0,2:T(2,128)(2,1)}), bf16[2,192,768]{1,0,2:T(2,128)(2,1)S(1)}, u32[]{:S(2)}, u32[]{:S(2)}) async-start(bf16[2,192,768]{1,0,2:T(2,128)(2,1)} %broadcast_select_fusion), calls=%async_computation.2 | async-start | bytes 1572864 | tf_op jit(solution)/shard_map/all_to_all | solution.py:119
  115.8 175.8 %while.20 = (s32[]{:T(128)}, f32[2,1536]{1,0:T(2,128)S(1)}, s32[7]{0:T(128)S(1)}, s32[]{:T(128)}, s32[768]{0:T(1024)S(1)}, /*index=5*/s32[]{:T(128)}, pred[]{:T(...) while((s32[]{:T(128)}, f32[2,1536]{1,0:T(2,128)S(1)}, ...), condition=%wide.region_3.4_spmd.clone, body=%wide.region_2.3_spmd.clone.sunk | while | flops 19283972 | bytes 4777152 | solution.py:73
  115.9 0.6 dynamic_slice.18
  117.1 0.6 broadcast_compare_fusion.3
  117.8 21.8 %cosine_convert_fusion.2 = (bf16[512,768]{1,0:T(8,128)(2,1)S(1)}, bf16[512,768]{1,0:T(8,128)(2,1)S(1)}) fusion(f32[]{:T(128)} %get-tuple-element.295, pred[]{:T(512)} %get-tuple-element.294, s32[]{:T(128)} %get-tuple-element.293, s32[768]{0:T(1024)S(1)} %get-tuple-element.292, s32[512]{0:T(512)S(1)} %iota_add_fusion.2), kind=kLoop, calls=%fused_computation.7.clone.1 | loop fusion | flops 5111808 | bytes 1577993 | tf_op jit(solution)/shard_map/convert
  139.6 0.5 convolution_bitcast_fusion.3
  140.1 0.6 fusion.38
  141.0 0.6 dynamic_slice.18
  142.2 0.6 broadcast_compare_fusion.3
  142.9 21.8 %cosine_convert_fusion.2 = (bf16[512,768]{1,0:T(8,128)(2,1)S(1)}, bf16[512,768]{1,0:T(8,128)(2,1)S(1)}) fusion(f32[]{:T(128)} %get-tuple-element.295, pred[]{:T(512)} %get-tuple-element.294, s32[]{:T(128)} %get-tuple-element.293, s32[768]{0:T(1024)S(1)} %get-tuple-element.292, s32[512]{0:T(512)S(1)} %iota_add_fusion.2), kind=kLoop, calls=%fused_computation.7.clone.1 | loop fusion | flops 5111808 | bytes 1577993 | tf_op jit(solution)/shard_map/convert
  164.7 0.5 convolution_bitcast_fusion.3
  165.2 0.6 fusion.38
  166.1 0.6 dynamic_slice.18
  167.3 0.6 broadcast_compare_fusion.3
  168.0 21.8 %cosine_convert_fusion.2 = (bf16[512,768]{1,0:T(8,128)(2,1)S(1)}, bf16[512,768]{1,0:T(8,128)(2,1)S(1)}) fusion(f32[]{:T(128)} %get-tuple-element.295, pred[]{:T(512)} %get-tuple-element.294, s32[]{:T(128)} %get-tuple-element.293, s32[768]{0:T(1024)S(1)} %get-tuple-element.292, s32[512]{0:T(512)S(1)} %iota_add_fusion.2), kind=kLoop, calls=%fused_computation.7.clone.1 | loop fusion | flops 5111808 | bytes 1577993 | tf_op jit(solution)/shard_map/convert
  189.8 0.5 convolution_bitcast_fusion.3
  190.3 0.6 fusion.38
  191.2 0.6 dynamic_slice.18
  192.5 0.6 broadcast_compare_fusion.3
  193.1 21.8 %cosine_convert_fusion.2 = (bf16[512,768]{1,0:T(8,128)(2,1)S(1)}, bf16[512,768]{1,0:T(8,128)(2,1)S(1)}) fusion(f32[]{:T(128)} %get-tuple-element.295, pred[]{:T(512)} %get-tuple-element.294, s32[]{:T(128)} %get-tuple-element.293, s32[768]{0:T(1024)S(1)} %get-tuple-element.292, s32[512]{0:T(512)S(1)} %iota_add_fusion.2), kind=kLoop, calls=%fused_computation.7.clone.1 | loop fusion | flops 5111808 | bytes 1577993 | tf_op jit(solution)/shard_map/convert
  214.9 0.5 convolution_bitcast_fusion.3
  215.4 0.6 fusion.38
  216.3 0.6 dynamic_slice.18
  217.6 0.6 broadcast_compare_fusion.3
  218.2 21.8 %cosine_convert_fusion.2 = (bf16[512,768]{1,0:T(8,128)(2,1)S(1)}, bf16[512,768]{1,0:T(8,128)(2,1)S(1)}) fusion(f32[]{:T(128)} %get-tuple-element.295, pred[]{:T(512)} %get-tuple-element.294, s32[]{:T(128)} %get-tuple-element.293, s32[768]{0:T(1024)S(1)} %get-tuple-element.292, s32[512]{0:T(512)S(1)} %iota_add_fusion.2), kind=kLoop, calls=%fused_computation.7.clone.1 | loop fusion | flops 5111808 | bytes 1577993 | tf_op jit(solution)/shard_map/convert
  240.0 0.5 convolution_bitcast_fusion.3
  240.5 0.6 fusion.38
  241.1 0.3 convolution_add_fusion.2
  241.4 0.6 dynamic_slice.18
  242.7 0.6 broadcast_compare_fusion.3
  243.3 21.8 %cosine_convert_fusion.2 = (bf16[512,768]{1,0:T(8,128)(2,1)S(1)}, bf16[512,768]{1,0:T(8,128)(2,1)S(1)}) fusion(f32[]{:T(128)} %get-tuple-element.295, pred[]{:T(512)} %get-tuple-element.294, s32[]{:T(128)} %get-tuple-element.293, s32[768]{0:T(1024)S(1)} %get-tuple-element.292, s32[512]{0:T(512)S(1)} %iota_add_fusion.2), kind=kLoop, calls=%fused_computation.7.clone.1 | loop fusion | flops 5111808 | bytes 1577993 | tf_op jit(solution)/shard_map/convert
  265.1 0.5 convolution_bitcast_fusion.3
  265.6 0.6 fusion.38
  266.6 0.6 dynamic_slice.18
  267.8 0.6 broadcast_compare_fusion.3
  268.5 21.8 %cosine_convert_fusion.2 = (bf16[512,768]{1,0:T(8,128)(2,1)S(1)}, bf16[512,768]{1,0:T(8,128)(2,1)S(1)}) fusion(f32[]{:T(128)} %get-tuple-element.295, pred[]{:T(512)} %get-tuple-element.294, s32[]{:T(128)} %get-tuple-element.293, s32[768]{0:T(1024)S(1)} %get-tuple-element.292, s32[512]{0:T(512)S(1)} %iota_add_fusion.2), kind=kLoop, calls=%fused_computation.7.clone.1 | loop fusion | flops 5111808 | bytes 1577993 | tf_op jit(solution)/shard_map/convert
  290.2 0.5 convolution_bitcast_fusion.3
  290.8 0.6 fusion.38
  291.3 0.3 convolution_add_fusion.2
  291.7 0.4 copy.56
  292.2 1.1 reshape.136
  293.3 3.2 all-to-all-start.1
  296.5 1.0 copy.58
  297.5 3.7 %all-to-all-done.1 = bf16[4,2,384]{2,1,0:T(2,128)(2,1)S(1)} async-done(((bf16[4,2,384]{2,1,0:T(2,128)(2,1)}), bf16[4,2,384]{2,1,0:T(2,128)(2,1)S(1)}, u32[]{:S(2)}, u32[]{:S(2)}) %all-to-all-start.1) | async-done | bytes 6176 | tf_op jit(solution)/shard_map/all_to_all | solution.py:117
  301.1 0.8 reshape.137
  302.0 0.3 copy.57
  302.3 14.4 %all_gather.7 = bf16[16,2,2,2,192]{4,3,2,1,0:T(2,128)(2,1)S(1)} all-gather(bf16[2,2,2,2,192]{4,3,2,1,0:T(2,128)(2,1)S(1)} %bitcast.68), channel_id=1, replica_groups=mesh['lat'=8,'wave'=4] {'lat'}, dimensions={0}, use_global_device_ids=true | all-gather | bytes 55296 | tf_op jit(solution)/shard_map/all_gather | solution.py:124
  316.7 0.4 copy.59
  317.2 0.7 convolution_bitcast_fusion.1
  317.9 1.0 copy.60
  (37 shorter events, 2.1 us)
Async XLA Ops:
  6.5 2.2 copy-start
  6.5 2.9 copy-start.1
  6.5 56.4 %all-gather.2.cloned.1.call-start = ((), (), s32[]{:S(2)}) async-start(), calls=%async_computation.3 | async-start | bytes 5308416 | tf_op jit(solution)/shard_map/all_gather | solution.py:102
  9.6 2.9 copy-start.4
  79.6 27.8 %copy-start.2 = (f32[2]{0:T(128)S(1)}, f32[2]{0:T(128)}, u32[]{:S(2)}) copy-start(f32[2]{0:T(128)} %param.13) | copy-start | bytes 28
  79.6 27.8 %copy-start.3 = (f32[2]{0:T(128)S(1)}, f32[2]{0:T(128)}, u32[]{:S(2)}) copy-start(f32[2]{0:T(128)} %param.12) | copy-start | bytes 28
  103.8 8.3 %all-to-all-start = ((bf16[4,3,2,192]{3,2,1,0:T(2,128)(2,1)}), bf16[4,3,2,192]{3,2,1,0:T(2,128)(2,1)S(1)}, u32[]{:S(2)}, u32[]{:S(2)}) async-start(bf16[4,3,2,192]{3,2,1,0:T(2,128)(2,1)} %bitcast.2), calls=%async_computation | async-start | bytes 24576 | tf_op jit(solution)/shard_map/all_to_all | solution.py:106
  112.1 181.1 %all-to-all-start.2 = ((bf16[2,192,768]{1,0,2:T(2,128)(2,1)}), bf16[2,192,768]{1,0,2:T(2,128)(2,1)S(1)}, u32[]{:S(2)}, u32[]{:S(2)}) async-start(bf16[2,192,768]{1,0,2:T(2,128)(2,1)} %broadcast_select_fusion), calls=%async_computation.2 | async-start | bytes 1572864 | tf_op jit(solution)/shard_map/all_to_all | solution.py:119
  293.3 7.9 %all-to-all-start.1 = ((bf16[4,2,384]{2,1,0:T(2,128)(2,1)}), bf16[4,2,384]{2,1,0:T(2,128)(2,1)S(1)}, u32[]{:S(2)}, u32[]{:S(2)}) async-start(bf16[4,2,384]{2,1,0:T(2,128)(2,1)} %reshape.136), calls=%async_computation.1 | async-start | bytes 12288 | tf_op jit(solution)/shard_map/all_to_all | solution.py:117
Sparse Core Ops, SparseCore 0:
  9.0 53.9 all-gather.1
where the time goes:
time: 327 us; the launch traced here: 326 us
  other arithmetic  167 us (51%)
  waiting for transfers between devices  52.1 us (16%)
  local copies, waits for them, and re-layouts  31.6 us (10%)
  matrix products  29.6 us (9%)
  between operations  16.2 us (5%)
  blocking collectives  14.4 us (4%)
  starting transfers between devices  10.4 us (3%)
  loops' own time  4.72 us (1%)
    another operation x8, other arithmetic  153 us
    all_gather x1, waiting for transfers between devices, local(): lax.all_gather(spectra, 'lat', axis=4, tiled=True)  47 us
    dot_general x1, matrix products, local(): jnp.einsum('lsn,fvpsn->lvfps', band_part, lax.all_gather(spectra, 'lat',...  23.1 us
    all_gather x1, local copies, waits for them, and re-layouts, local(): lax.all_gather(spectra, 'lat', axis=4, tiled=True)  16.6 us
    all_gather x1, blocking collectives, local(): lax.all_gather(returned, 'lat', axis=0, tiled=True)  14.4 us
  transfers between devices with their start and end apart: 4, of which 3 were waited for; matrix products, arithmetic and copies ran while one was open for 56% of the time, Pallas kernels for 0%

commit v1 on v0

v1 whole, which is shorter than its diff:
```python
import functools
import math

import jax
import jax.numpy as jnp
from jax import lax
from jax.experimental import pallas as pl
from jax.experimental.pallas import tpu as pltpu
from jax.sharding import PartitionSpec as P

NLON = 3088
BASE = 32

F32 = jnp.float32
BF16 = jnp.bfloat16


def whole(memory_space=pltpu.VMEM):
    return pl.BlockSpec(memory_space=memory_space)


def turn_kernel(ids_ref, legendre_ref, out_ref):
    total, columns = out_ref.shape
    ids = ids_ref[...]
    for first in range(0, total, 128):
        piece = legendre_ref[:, first : first + 128].astype(F32).T
        degrees = first + lax.broadcasted_iota(jnp.int32, piece.shape, 0)
        out_ref[first : first + 128, :] = jnp.where(degrees >= ids, piece, 0.0).astype(BF16)


def turn_spectra_kernel(repeats, spectra_ref, out_ref):
    slots = spectra_ref.shape[1]
    for i in range(spectra_ref.shape[0]):
        turned = spectra_ref[i].astype(F32).T
        out_ref[i] = jnp.concatenate([turned] * repeats, axis=1)


def forward_kernel(legendre_ref, spectra_ref, out_ref):
    sources, degrees, columns = legendre_ref.shape
    fields = spectra_ref.shape[0]

    def one_source(a, carry):
        piece = legendre_ref[a].astype(F32)
        rows = [
            jnp.sum(piece * spectra_ref[i], axis=0, keepdims=True) for i in range(fields)
        ]
        out_ref[a] = jnp.concatenate(rows, axis=0).astype(BF16)
        return carry

    lax.fori_loop(0, sources, one_source, 0)


def cos_sin(places, ids, count, inverse):
    quads = 4.0 * places * ids
    turns = jnp.floor(quads * inverse + 0.5)
    angle = (quads - turns * count) * (inverse * (math.pi / 2))
    square = angle * angle
    c = 1.0 + square * (-1 / 2 + square * (1 / 24 + square * (-1 / 720 + square * (1 / 40320))))
    s = angle * (
        1.0 + square * (-1 / 6 + square * (1 / 120 + square * (-1 / 5040 + square * (1 / 362880))))
    )
    quadrant = turns - 4.0 * jnp.floor(turns * 0.25)
    odd = (quadrant == 1.0) | (quadrant == 3.0)
    cosine = jnp.where(odd, s, c)
    sine = jnp.where(odd, c, s)
    cosine = jnp.where((quadrant == 1.0) | (quadrant == 2.0), -cosine, cosine)
    sine = jnp.where(quadrant >= 2.0, -sine, sine)
    return cosine, sine


def grid_kernel(
    lev_count, rank_ref, nlon_ref, coriolis_ref, weight_ref, fourier_ref, ids_ref, out_ref,
    base_ref, step_ref, table_ref, left_ref,
):
    owned, _, waves = fourier_ref.shape
    steps = step_ref.shape[1]
    places = BASE * steps
    ids = ids_ref[...].astype(F32)
    parity = 1.0 - 2.0 * (ids - 2.0 * jnp.floor(ids * 0.5))
    for offset in range(owned):
        latitude = (rank_ref[0] * owned + offset) // lev_count
        count_int = nlon_ref[latitude]
        count = jnp.full((1, waves), count_int.astype(F32))
        inverse = 1.0 / count
        rows = lax.broadcasted_iota(jnp.int32, (BASE, waves), 0).astype(F32)
        base_ref[0], base_ref[1] = cos_sin(rows, ids, count, inverse)
        rows = lax.broadcasted_iota(jnp.int32, (steps, waves), 0).astype(F32) * BASE
        step_ref[0], step_ref[1] = cos_sin(rows, ids, count, inverse)
        for a in range(steps):
            step_c = step_ref[0, a : a + 1, :]
            step_s = step_ref[1, a : a + 1, :]
            base_c = base_ref[0]
            base_s = base_ref[1]
            here = slice(a * BASE, (a + 1) * BASE)
            table_ref[here, :waves] = (step_c * base_c - step_s * base_s).astype(BF16)
            table_ref[here, waves:] = (step_s * base_c + step_c * base_s).astype(BF16)

        factor = jnp.where(ids == 0.0, 1.0, 2.0)
        factor = jnp.where(2.0 * ids < count, factor, 0.0)
        for field in range(3):
            real = fourier_ref[offset, 2 * field : 2 * field + 1, :].astype(F32) * factor
            imag = -fourier_ref[offset, 2 * field + 1 : 2 * field + 2, :].astype(F32) * factor
            first = jnp.concatenate([real, real, real * parity, real * parity], axis=0)
            second = jnp.concatenate([imag, -imag, -imag * parity, imag * parity], axis=0)
            pad = jnp.zeros((4, waves), F32)
            left_ref[8 * field : 8 * field + 8, :waves] = jnp.concatenate([first, pad], axis=0)
            left_ref[8 * field : 8 * field + 8, waves:] = jnp.concatenate([second, pad], axis=0)
        grid = lax.dot_general(
            left_ref[...].astype(BF16),
            table_ref[...],
            (((1,), (1,)), ((), ())),
            preferred_element_type=F32,
        )
        vorticity, divergence, temperature = grid[0:8], grid[8:16], grid[16:24]
        stretch = -(vorticity + coriolis_ref[latitude]) * divergence
        heating = -temperature * divergence
        quarter = count_int // 4
        place = lax.broadcasted_iota(jnp.int32, stretch.shape, 1)
        share = jnp.where((place == 0) | (place == quarter), 0.5, 1.0)

        def shared(product):
            rounded = jnp.where(place <= quarter, product, 0.0).astype(BF16)
            return rounded.astype(F32) * share

        products = jnp.concatenate([shared(stretch), shared(heating)], axis=0).astype(BF16)
        sums = jnp.dot(products, table_ref[...], preferred_element_type=F32)
        scale = weight_ref[latitude] / count
        for q in range(2):
            c = sums[8 * q : 8 * q + 4, :waves]
            s = sums[8 * q : 8 * q + 4, waves:]
            real = (c[0:1] + c[1:2]) + parity * (c[2:3] + c[3:4])
            imag = (s[0:1] - s[1:2]) + parity * (s[3:4] - s[2:3])
            both = jnp.concatenate([real * scale, -imag * scale], axis=0)
            both = jnp.where(factor > 0.0, both, 0.0).astype(BF16)
            out_ref[offset, 2 * q : 2 * q + 2, :] = both


def backward_kernel(lats, legendre_ref, back_ref, out_ref, turned_ref):
    sources, degrees, columns = legendre_ref.shape
    outs = back_ref.shape[1]
    slots = columns // lats
    for first in range(0, degrees, 8):
        last = min(first + 8, degrees)

        def one_source(a, sums):
            piece = legendre_ref[a, first:last, :].astype(F32)
            return tuple(
                total + piece * back_ref[a, i : i + 1, :] for i, total in enumerate(sums)
            )

        zero = jnp.zeros((last - first, columns), F32)
        sums = lax.fori_loop(0, sources, one_source, (zero,) * outs)
        for i in range(outs):
            folded = sums[i][:, :slots]
            for lat in range(1, lats):
                folded = folded + sums[i][:, lat * slots : (lat + 1) * slots]
            turned_ref[i, first:last, :] = folded
    for i in range(outs):
        out_ref[i] = turned_ref[i].T


def local(n_lat, n_wave, spectra, legendre, wave_m, nlon, coriolis, gauss_quadrature_weight):
    lats, slots, total = legendre.shape
    levels = spectra.shape[1]
    waves = wave_m.shape[0]
    degrees = spectra.shape[4]
    columns = lats * slots
    owned = lats * levels // n_wave
    wave_rank = lax.axis_index("wave")
    ids = lax.dynamic_slice_in_dim(wave_m, wave_rank * slots, slots, 0)
    ids = jnp.tile(ids, lats).reshape(1, columns)

    turned = pl.pallas_call(
        turn_kernel,
        out_shape=jax.ShapeDtypeStruct((total, columns), BF16),
        in_specs=[whole(), whole()],
        out_specs=whole(),
        name="turn",
    )(ids, legendre.reshape(columns, total))
    turned = lax.all_to_all(turned.reshape(n_lat, degrees, columns), "lat", 0, 0, tiled=True)

    spectra_turned = pl.pallas_call(
        functools.partial(turn_spectra_kernel, lats),
        out_shape=jax.ShapeDtypeStruct((6 * levels, degrees, columns), F32),
        in_specs=[whole()],
        out_specs=whole(),
        name="turn_spectra",
    )(spectra.reshape(6 * levels, slots, degrees))

    partial = pl.pallas_call(
        forward_kernel,
        out_shape=jax.ShapeDtypeStruct((n_lat, 6 * levels, columns), BF16),
        in_specs=[whole(), whole()],
        out_specs=whole(),
        name="forward",
    )(turned, spectra_turned)

    partial = partial.reshape(n_lat, 3, levels, 2, lats, slots).transpose(0, 4, 2, 1, 3, 5)
    partial = partial.reshape(n_lat * n_wave, owned, 6, slots)
    gathered = lax.all_to_all(partial, ("lat", "wave"), 0, 0, tiled=True)
    gathered = gathered.reshape(n_lat, n_wave, owned, 6, slots).astype(F32).sum(axis=0)
    fourier = gathered.transpose(1, 2, 0, 3).reshape(owned, 6, waves).astype(BF16)

    quarter_places = NLON // 4 + 1
    steps = -(-quarter_places // BASE)
    smem = whole(pltpu.SMEM)
    back = pl.pallas_call(
        functools.partial(grid_kernel, levels),
        out_shape=jax.ShapeDtypeStruct((owned, 4, waves), BF16),
        in_specs=[smem, smem, smem, smem, whole(), whole()],
        out_specs=whole(),
        scratch_shapes=[
            pltpu.VMEM((2, BASE, waves), F32),
            pltpu.VMEM((2, steps, waves), F32),
            pltpu.VMEM((steps * BASE, 2 * waves), BF16),
            pltpu.VMEM((24, 2 * waves), F32),
        ],
        name="grid",
    )(
        wave_rank.reshape(1),
        nlon,
        coriolis,
        gauss_quadrature_weight,
        fourier,
        wave_m.reshape(1, waves),
    )

    back = back.reshape(owned, 4, n_wave, slots).transpose(2, 0, 1, 3)
    back = jnp.broadcast_to(back[None], (n_lat,) + back.shape)
    back = back.reshape(n_lat * n_wave, owned, 4, slots)
    back = lax.all_to_all(back, ("lat", "wave"), 0, 0, tiled=True)
    back = back.reshape(n_lat, lats, levels, 2, 2, slots).transpose(0, 3, 2, 4, 1, 5)
    back = back.reshape(n_lat, 4 * levels, columns).astype(F32)

    out = pl.pallas_call(
        functools.partial(backward_kernel, lats),
        out_shape=jax.ShapeDtypeStruct((4 * levels, slots, degrees), F32),
        in_specs=[whole(), whole()],
        out_specs=whole(),
        scratch_shapes=[pltpu.VMEM((4 * levels, degrees, slots), F32)],
        name="backward",
    )(turned, back)
    return out.reshape(2, levels, 2, slots, degrees)


def solution(mesh):
    placed = (
        P(None, None, None, "wave", "lat"),
        P("lat", "wave", None),
        P(),
        P("lat"),
        P("lat"),
        P("lat"),
    )
    return jax.shard_map(
        functools.partial(local, mesh.shape["lat"], mesh.shape["wave"]),
        mesh=mesh,
        in_specs=placed,
        out_specs=P(None, None, None, "wave", "lat"),
        check_vma=False,
    )
```

time: 327 us -> 64.9 us (0.20)
  other arithmetic: 167 us -> 0.05 us
  waiting for transfers between devices: 52.1 us -> 21.8 us
  matrix products: 29.6 us -> 0 us
  local copies, waits for them, and re-layouts: 31.6 us -> 7.09 us
  Pallas kernels: 0 us -> 16.2 us
  between operations: 16.2 us -> 0.08 us
  blocking collectives: 14.4 us -> 9.19 us
  loops' own time: 4.72 us -> 0 us
    another operation x16 -> x0, other arithmetic: 157 us -> none
    all_gather x1 -> x0, waiting for transfers between devices: 47 us -> none  [local(): lax.all_gather(spectra, 'lat', axis=4, tiled=True)]
    dot_general x16 -> x0, matrix products: 29.6 us -> none  [the longest x1 23.1 us: local(): jnp.einsum('lsn,fvpsn->lvfps', band_part, lax.all_gather(spectra, 'lat',...]
    all_gather x2 -> x0, local copies, waits for them, and re-layouts: 17.1 us -> none  [the longest x1 16.6 us: local(): lax.all_gather(spectra, 'lat', axis=4, tiled=True)]
    all_to_all x3 -> x2, waiting for transfers between devices: 5.13 us -> 21.8 us  [the longest x1 14 us: local(): lax.all_to_all(turned.reshape(n_lat, degrees, columns), 'lat', 0, 0, tile...]
    pallas_call x0 -> x5, Pallas kernels: none -> 16.2 us  [the longest x1 4.6 us: local(): pl.pallas_call(functools.partial(backward_kernel, lats), out_shape=jax.Sh...]
    all_gather x1 -> x0, blocking collectives: 14.4 us -> none  [local(): lax.all_gather(returned, 'lat', axis=0, tiled=True)]
    all_to_all x0 -> x1, blocking collectives: none -> 9.19 us  [local(): back = lax.all_to_all(back, ('lat', 'wave'), 0, 0, tiled=True)]
  transfers between devices with their start and end apart: 4 -> 2, of which waited for: 3 -> 2; matrix products, arithmetic and copies ran while one was open for 56% -> 1% of each run, Pallas kernels for 0% -> 4%
where the time goes in v1:
time: 64.9 us; the launch traced here: 64.3 us
  waiting for transfers between devices  21.8 us (34%)
  Pallas kernels  16.2 us (25%)
  starting transfers between devices  9.89 us (15%)
  blocking collectives  9.19 us (14%)
  local copies, waits for them, and re-layouts  7.09 us (11%)
    all_to_all x1, waiting for transfers between devices, local(): lax.all_to_all(turned.reshape(n_lat, degrees, columns), 'lat', 0, 0, tile...  14 us
    all_to_all x1, blocking collectives, local(): back = lax.all_to_all(back, ('lat', 'wave'), 0, 0, tiled=True)  9.19 us
    all_to_all x1, waiting for transfers between devices, local(): gathered = lax.all_to_all(partial, ('lat', 'wave'), 0, 0, tiled=True)  7.77 us
    all_to_all x1, starting transfers between devices, local(): lax.all_to_all(turned.reshape(n_lat, degrees, columns), 'lat', 0, 0, tile...  6.35 us
    pallas_call x1, Pallas kernels, local(): pl.pallas_call(functools.partial(backward_kernel, lats), out_shape=jax.Sh...  4.6 us
    pallas_call x1, Pallas kernels, local(): pl.pallas_call(forward_kernel, out_shape=jax.ShapeDtypeStruct((n_lat, 6 *...  3.61 us
    all_to_all x1, starting transfers between devices, local(): gathered = lax.all_to_all(partial, ('lat', 'wave'), 0, 0, tiled=True)  3.54 us
    pallas_call x1, Pallas kernels, local(): pl.pallas_call(functools.partial(grid_kernel, levels), out_shape=jax.Shap...  3.17 us
  transfers between devices with their start and end apart: 2, of which 2 were waited for; matrix products, arithmetic and copies ran while one was open for 1% of the time, Pallas kernels for 4%

profile of v1, /device:TPU:0, one launch (start us, length us, event | category | flops | bytes accessed | tf_op | source)
XLA Modules:
  0.0 64.3 jit_solution(14967663116082026490)
XLA Ops:
  0.0 0.8 %dynamic_slice.3 = s32[192]{0:T(256)S(1)} dynamic-slice(s32[768]{0:T(1024)} %param.8, s32[]{:T(128)S(6)} %select_n.3), dynamic_slice_sizes={192} | dynamic-slice | bytes 1540 | tf_op jit(solution)/shard_map/dynamic_slice | solution.py:170
  0.8 0.6 reshape_tile.3.ids_ref
  1.4 2.1 %turn.1 = bf16[768,384]{1,0:T(8,128)(2,1)} custom-call(s32[1,384]{1,0:T(1,128)} %reshape_tile.3.ids_ref, bf16[384,768]{1,0:T(8,128)(2,1)} %bitcast.24), custom_call_target="tpu_custom_call" | custom-call | tf_op jit(solution)/shard_map/turn/pallas_call | solution.py:173
  3.5 6.4 %all-to-all-start = ((bf16[8,96,384]{2,1,0:T(8,128)(2,1)}), bf16[8,96,384]{2,1,0:T(8,128)(2,1)S(1)}, u32[]{:S(2)}, u32[]{:S(2)}) async-start(bf16[8,96,384]{2,1,0:T(8,128)(2,1)} %bitcast.23), calls=%async_computation | async-start | bytes 1179648 | tf_op jit(solution)/shard_map/all_to_all | solution.py:180
  9.9 2.7 %turn_spectra.1.spectra_ref = f32[12,96,384]{2,1,0:T(8,128)} custom-call(bf16[12,192,96]{2,1,0:T(8,128)(2,1)} %bitcast.25), custom_call_target="tpu_custom_call" | custom-call | tf_op jit(solution)/shard_map/turn_spectra/pallas_call | solution.py:182
  12.6 0.0 copy-start.1
  12.6 14.0 %all-to-all-done.legendre_ref = bf16[8,96,384]{2,1,0:T(8,128)(2,1)S(1)} async-done(((bf16[8,96,384]{2,1,0:T(8,128)(2,1)}), bf16[8,96,384]{2,1,0:T(8,128)(2,1)S(1)}, u32[]{:S(2)}, u32[]{:S(2)}) %all-to-all-start) | async-done | bytes 589856 | tf_op jit(solution)/shard_map/all_to_all | solution.py:180
  26.6 0.0 copy-start
  26.6 0.8 %copy-done = bf16[8,96,384]{2,1,0:T(8,128)(2,1)} copy-done((bf16[8,96,384]{2,1,0:T(8,128)(2,1)}, bf16[8,96,384]{2,1,0:T(8,128)(2,1)S(1)}, u32[]{:S(2)}) %copy-start) | copy-done | bytes 589848
  27.5 3.6 %forward.1 = bf16[8,12,384]{2,1,0:T(8,128)(2,1)} custom-call(bf16[8,96,384]{2,1,0:T(8,128)(2,1)} %copy-done, f32[12,96,384]{2,1,0:T(8,128)} %turn_spectra.1.spectra_ref), custom_call_target="tpu_custom_call" | custom-call | tf_op jit(solution)/shard_map/forward/pallas_call | solution.py:190
  31.1 0.9 %copy.24 = bf16[8,12,384]{2,0,1:T(8,128)(2,1)S(1)} copy(bf16[8,12,384]{2,1,0:T(8,128)(2,1)} %forward.1) | data formatting | bytes 147456 | tf_op jit(solution)/shard_map/forward/pallas_call | solution.py:190
  32.0 0.1 reshape.77
  32.1 0.1 copy.31
  32.2 0.8 %reshape.84 = bf16[32,1,6,192]{3,2,1,0:T(8,128)(2,1)} reshape(bf16[8,2,2,3,2,192]{5,4,3,2,1,0:T(2,128)(2,1)S(1)} %copy.31) | data formatting | bytes 147456 | tf_op jit(solution)/shard_map/reshape | solution.py:199
  32.9 3.5 %all-to-all-start.1 = ((bf16[32,1,6,192]{3,2,1,0:T(8,128)(2,1)}), bf16[32,1,6,192]{3,2,1,0:T(8,128)(2,1)S(1)}, u32[]{:S(2)}, u32[]{:S(2)}) async-start(bf16[32,1,6,192]{3,2,1,0:T(8,128)(2,1)} %reshape.84), calls=%async_computation.1 | async-start | bytes 262144 | tf_op jit(solution)/shard_map/all_to_all | solution.py:200
  36.5 0.0 copy-done.1
  36.5 0.6 reshape.79.ids_ref
  37.1 7.8 %all-to-all-done.1 = bf16[32,1,6,192]{3,2,1,0:T(8,128)(2,1)S(1)} async-done(((bf16[32,1,6,192]{3,2,1,0:T(8,128)(2,1)}), bf16[32,1,6,192]{3,2,1,0:T(8,128)(2,1)S(1)}, u32[]{:S(2)}, u32[]{:S(2)}) %all-to-all-start.1) | async-done | bytes 73760 | tf_op jit(solution)/shard_map/all_to_all | solution.py:200
  44.9 0.7 %convert_element_type.40.fourier_ref = bf16[1,6,768]{2,1,0:T(8,128)(2,1)} reshape(bf16[1,6,4,192]{3,2,1,0:T(4,128)(2,1)S(1)} %copy.27) | data formatting | bytes 18432 | tf_op jit(solution)/shard_map/convert_element_type | solution.py:202
  45.6 3.2 %grid.1 = bf16[1,4,768]{2,1,0:T(4,128)(2,1)} custom-call(s32[1]{0:T(128)} %bitcast.2.rank_ref, s32[2]{0:T(128)} %nlon_ref.1, f32[2]{0:T(128)} %coriolis_ref.1, f32[2]{0:T(128)} %weight_ref.1, bf16[1,6,768]{2,1,0:T(8,128)(2,1)} %convert_element_type.40.fourier_ref, s32[1,768]{1,0:T(1,128)} %reshape.79.ids_ref), custom_call_target="tpu_custom_call" | custom-call | tf_op jit(solution)/shard_map/grid/pallas_call | solution.py:207
  48.8 0.8 %reshape.80 = bf16[1,4,4,192]{3,2,1,0:T(4,128)(2,1)S(1)} reshape(bf16[1,4,768]{2,1,0:T(4,128)(2,1)} %grid.1) | data formatting | bytes 12288 | tf_op jit(solution)/shard_map/reshape | solution.py:228
  49.6 9.2 %all_to_all.15 = bf16[32,1,4,192]{3,2,1,0:T(4,128)(2,1)S(1)} all-to-all(bf16[32,1,4,192]{3,2,1,0:T(4,128)(2,1)S(1)} %bitcast.29), channel_id=1, replica_groups=mesh['lat'=8,'wave'=4] {'lat','wave'}, dimensions={0} | all-to-all | bytes 98304 | tf_op jit(solution)/shard_map/all_to_all | solution.py:231
  58.8 0.1 reshape.83
  58.9 0.1 copy.30
  59.0 0.8 %reshape.82.back_ref = f32[8,8,384]{2,1,0:T(8,128)} reshape(f32[8,2,2,2,2,192]{5,4,3,2,1,0:T(2,128)S(1)} %copy.30) | data formatting | bytes 196608 | tf_op jit(solution)/shard_map/convert_element_type | solution.py:233
  59.7 4.6 %backward.1 = f32[8,192,96]{2,1,0:T(8,128)} custom-call(bf16[8,96,384]{2,1,0:T(8,128)(2,1)} %copy-done, f32[8,8,384]{2,1,0:T(8,128)} %reshape.82.back_ref), custom_call_target="tpu_custom_call" | custom-call | tf_op jit(solution)/shard_map/backward/pallas_call | solution.py:235
  (6 shorter events, 0.1 us)
Async XLA Ops:
  3.5 23.1 %all-to-all-start = ((bf16[8,96,384]{2,1,0:T(8,128)(2,1)}), bf16[8,96,384]{2,1,0:T(8,128)(2,1)S(1)}, u32[]{:S(2)}, u32[]{:S(2)}) async-start(bf16[8,96,384]{2,1,0:T(8,128)(2,1)} %bitcast.23), calls=%async_computation | async-start | bytes 1179648 | tf_op jit(solution)/shard_map/all_to_all | solution.py:180
  12.6 23.9 %copy-start.1 = (s32[768]{0:T(1024)S(1)}, s32[768]{0:T(1024)}, u32[]{:S(2)}) copy-start(s32[768]{0:T(1024)} %param.8) | copy-start | bytes 9220
  26.6 0.8 %copy-start = (bf16[8,96,384]{2,1,0:T(8,128)(2,1)}, bf16[8,96,384]{2,1,0:T(8,128)(2,1)S(1)}, u32[]{:S(2)}) copy-start(bf16[8,96,384]{2,1,0:T(8,128)(2,1)S(1)} %all-to-all-done.legendre_ref) | copy-start | bytes 1769476
  32.9 11.9 %all-to-all-start.1 = ((bf16[32,1,6,192]{3,2,1,0:T(8,128)(2,1)}), bf16[32,1,6,192]{3,2,1,0:T(8,128)(2,1)S(1)}, u32[]{:S(2)}, u32[]{:S(2)}) async-start(bf16[32,1,6,192]{3,2,1,0:T(8,128)(2,1)} %reshape.84), calls=%async_computation.1 | async-start | bytes 262144 | tf_op jit(solution)/shard_map/all_to_all | solution.py:200

commit v2 on v1

v2 whole, which is shorter than its diff:
```python
import functools
import math

import jax
import jax.numpy as jnp
from jax import lax
from jax.experimental import pallas as pl
from jax.experimental.pallas import tpu as pltpu
from jax.sharding import PartitionSpec as P

NLON = 3088
BASE = 32
LANES = 128

F32 = jnp.float32
BF16 = jnp.bfloat16

VMEM = pl.BlockSpec(memory_space=pltpu.VMEM)
SMEM = pl.BlockSpec(memory_space=pltpu.SMEM)
ANY = pl.BlockSpec(memory_space=pl.ANY)


def call(body, name, out_shape, in_specs, scratch=(), out_specs=VMEM, flops=0, bytes_accessed=0):
    return pl.pallas_call(
        body,
        out_shape=out_shape,
        in_specs=in_specs,
        out_specs=out_specs,
        scratch_shapes=scratch,
        name=name,
        cost_estimate=pl.CostEstimate(
            flops=flops, bytes_accessed=bytes_accessed, transcendentals=0
        ),
        compiler_params=pltpu.CompilerParams(vmem_limit_bytes=16 * 1024 * 1024),
    )


def pieces(extent, size):
    return [(first, min(first + size, extent)) for first in range(0, extent, size)]


def turn_kernel(legendre_ref, out_ref, held_ref, sems):
    parts = pieces(legendre_ref.shape[1], LANES)
    copies = []
    for i, (first, last) in enumerate(parts):
        copies.append(
            pltpu.make_async_copy(
                legendre_ref.at[:, first:last], held_ref.at[:, first:last], sems.at[i]
            )
        )
        copies[-1].start()
    for i, (first, last) in enumerate(parts):
        copies[i].wait()
        out_ref[first:last, :] = held_ref[:, first:last].T


def turn_spectra_kernel(repeats, fields, rank_ref, spectra_ref, ids_ref, out_ref):
    count, slots, degrees = spectra_ref.shape
    levels = count // (2 * fields)
    degree = rank_ref[0] * degrees + lax.broadcasted_iota(jnp.int32, (degrees, slots), 0)
    alive = degree >= ids_ref[...]
    for i in range(count):
        field, level, part = i // (2 * levels), (i // 2) % levels, i % 2
        turned = jnp.where(alive, spectra_ref[i].astype(F32).T, 0.0)
        place = (level * fields + field) * 2 + part
        out_ref[place] = jnp.concatenate([turned] * repeats, axis=1)


def forward_kernel(levels, owned, legendre_ref, spectra_ref, out_ref):
    sources, degrees, columns = legendre_ref.shape
    fields = spectra_ref.shape[0]
    per_level = fields // levels
    slots = out_ref.shape[-1]
    lats = columns // slots
    targets = out_ref.shape[0] // sources
    group = 2 if sources % 2 == 0 else 1

    def fold(value):
        total = value[0:8] if value.shape[0] >= 8 else value
        for first, last in pieces(value.shape[0], 8)[1:]:
            if last - first == 8:
                total = total + value[first:last]
        return total

    def some_sources(g, carry):
        tiles = [[] for _ in range(group)]
        for left, right in pieces(columns, LANES):
            sums = [[None] * fields for _ in range(group)]
            for first, last in pieces(degrees, 16):
                own = [
                    legendre_ref[g * group + k, first:last, left:right].astype(F32)
                    for k in range(group)
                ]
                for i in range(fields):
                    other = spectra_ref[i, first:last, left:right]
                    for k in range(group):
                        product = own[k] * other
                        rest = product.shape[0] % 8
                        if product.shape[0] > 8 and rest == 0:
                            product = fold(product)
                        else:
                            product = jnp.sum(product, axis=0, keepdims=True)
                        sums[k][i] = product if sums[k][i] is None else sums[k][i] + product
            for k in range(group):
                rows = [jnp.sum(value, axis=0, keepdims=True) for value in sums[k]]
                tiles[k].append(jnp.concatenate(rows, axis=0))
        for k in range(group):
            whole = jnp.concatenate(tiles[k], axis=1)
            for row in range(lats * levels):
                lat, level = row // levels, row % levels
                out_ref[(g * group + k) * targets + row // owned, row % owned] = whole[
                    level * per_level : (level + 1) * per_level,
                    lat * slots : (lat + 1) * slots,
                ].astype(BF16)
        return carry

    lax.fori_loop(0, sources // group, some_sources, 0)


def cos_sin(places, ids, count, inverse):
    quads = 4.0 * places * ids
    turns = jnp.floor(quads * inverse + 0.5)
    angle = (quads - turns * count) * (inverse * (math.pi / 2))
    square = angle * angle
    c = 1.0 + square * (-1 / 2 + square * (1 / 24 + square * (-1 / 720 + square * (1 / 40320))))
    s = angle * (
        1.0 + square * (-1 / 6 + square * (1 / 120 + square * (-1 / 5040 + square * (1 / 362880))))
    )
    quadrant = turns - 4.0 * jnp.floor(turns * 0.25)
    odd = (quadrant == 1.0) | (quadrant == 3.0)
    cosine = jnp.where(odd, s, c)
    sine = jnp.where(odd, c, s)
    cosine = jnp.where((quadrant == 1.0) | (quadrant == 2.0), -cosine, cosine)
    sine = jnp.where(quadrant >= 2.0, -sine, sine)
    return cosine, sine


def table_kernel(levels, rank_ref, nlon_ref, ids_ref, table_ref, base_ref, step_ref):
    owned = table_ref.shape[0]
    steps = step_ref.shape[1]
    waves = ids_ref.shape[1]
    ids = ids_ref[...].astype(F32)
    for offset in range(owned):
        latitude = (rank_ref[0] * owned + offset) // levels
        count = jnp.full((1, waves), nlon_ref[latitude].astype(F32))
        inverse = 1.0 / count
        rows = lax.broadcasted_iota(jnp.int32, (BASE, waves), 0).astype(F32)
        base_ref[0], base_ref[1] = cos_sin(rows, ids, count, inverse)
        rows = lax.broadcasted_iota(jnp.int32, (steps, waves), 0).astype(F32) * BASE
        step_ref[0], step_ref[1] = cos_sin(rows, ids, count, inverse)
        for a in range(steps):
            step_c = step_ref[0, a : a + 1, :]
            step_s = step_ref[1, a : a + 1, :]
            base_c = base_ref[0]
            base_s = base_ref[1]
            here = slice(a * BASE, (a + 1) * BASE)
            table_ref[offset, here, :waves] = (step_c * base_c - step_s * base_s).astype(BF16)
            table_ref[offset, here, waves:] = (step_s * base_c + step_c * base_s).astype(BF16)


def grid_kernel(
    levels, rank_ref, nlon_ref, coriolis_ref, weight_ref, partial_ref, table_ref, ids_ref, out_ref,
    left_ref,
):
    owned, _, slots = partial_ref.shape[1:]
    waves = ids_ref.shape[1]
    parts = waves // slots
    sources = partial_ref.shape[0] // parts
    ids = ids_ref[...].astype(F32)
    parity = 1.0 - 2.0 * (ids - 2.0 * jnp.floor(ids * 0.5))
    left_ref[...] = jnp.zeros_like(left_ref)
    for offset in range(owned):
        latitude = (rank_ref[0] * owned + offset) // levels
        count_int = nlon_ref[latitude]
        count = jnp.full((1, waves), count_int.astype(F32))

        def total(w):
            def add(a, value):
                return value + partial_ref[a * parts + w, offset].astype(F32)

            if sources > 8:
                return lax.fori_loop(1, sources, add, partial_ref[w, offset].astype(F32))
            value = partial_ref[w, offset].astype(F32)
            for a in range(1, sources):
                value = add(a, value)
            return value

        factor = jnp.where(ids == 0.0, 1.0, 2.0)
        factor = jnp.where(2.0 * ids < count, factor, 0.0)
        fourier = jnp.concatenate([total(w) for w in range(parts)], axis=1)
        fourier = fourier.astype(BF16).astype(F32) * factor
        for field in range(3):
            real = fourier[2 * field : 2 * field + 1]
            imag = -fourier[2 * field + 1 : 2 * field + 2]
            first = jnp.concatenate([real, real, real * parity, real * parity], axis=0)
            second = jnp.concatenate([imag, -imag, -imag * parity, imag * parity], axis=0)
            left_ref[8 * field : 8 * field + 4, :waves] = first
            left_ref[8 * field : 8 * field + 4, waves:] = second
        grid = lax.dot_general(
            left_ref[...].astype(BF16),
            table_ref[offset],
            (((1,), (1,)), ((), ())),
            preferred_element_type=F32,
        )
        vorticity, divergence, temperature = grid[0:8], grid[8:16], grid[16:24]
        stretch = -(vorticity + coriolis_ref[latitude]) * divergence
        heating = -temperature * divergence
        quarter = count_int // 4
        place = lax.broadcasted_iota(jnp.int32, stretch.shape, 1)
        share = jnp.where((place == 0) | (place == quarter), 0.5, 1.0)

        def shared(product):
            rounded = jnp.where(place <= quarter, product, 0.0).astype(BF16)
            return rounded.astype(F32) * share

        products = jnp.concatenate([shared(stretch), shared(heating)], axis=0).astype(BF16)
        sums = jnp.dot(products, table_ref[offset], preferred_element_type=F32)
        scale = weight_ref[latitude] / count
        both = []
        for q in range(2):
            c = sums[8 * q : 8 * q + 4, :waves]
            s = sums[8 * q : 8 * q + 4, waves:]
            real = (c[0:1] + c[1:2]) + parity * (c[2:3] + c[3:4])
            imag = (s[0:1] - s[1:2]) + parity * (s[3:4] - s[2:3])
            both += [real * scale, -imag * scale]
        back = jnp.concatenate(both, axis=0)
        back = jnp.where(factor > 0.0, back, 0.0).astype(BF16)
        for w in range(parts):
            part = back[:, w * slots : (w + 1) * slots]

            def put(a, carry):
                out_ref[a * parts + w, offset] = part
                return carry

            if sources > 8:
                lax.fori_loop(0, sources, put, 0)
            else:
                for a in range(sources):
                    put(a, 0)


def backward_kernel(
    levels, rank_ref, legendre_ref, back_ref, ids_ref, out_ref, wide_ref, sums_ref, done_ref, sems
):
    sources, degrees, columns = legendre_ref.shape
    outs, slots, _ = out_ref.shape
    lats = columns // slots
    owned = back_ref.shape[1]
    targets = back_ref.shape[0] // sources
    group = min(sources, 8)

    def spread(a, carry):
        for level in range(levels):
            rows = []
            for lat in range(lats):
                row = lat * levels + level
                rows.append(back_ref[a * targets + row // owned, row % owned].astype(F32))
            both = jnp.concatenate(rows, axis=1)
            for i in range(4):
                place = ((i // 2) * levels + level) * 2 + i % 2
                wide_ref[a, place] = jnp.broadcast_to(both[i : i + 1], (8, columns))
        return carry

    if sources > 8:
        lax.fori_loop(0, sources, spread, 0)
    else:
        for a in range(sources):
            spread(a, 0)

    for first, last in pieces(degrees, 16):
        for left, right in pieces(columns, LANES):

            def some_sources(g, sums):
                sums = list(sums)
                for k in range(group):
                    piece = legendre_ref[g * group + k, first:last, left:right].astype(F32)
                    for i in range(outs):
                        other = wide_ref[g * group + k, i, :, left:right]
                        other = jnp.concatenate([other, other], axis=0)[: last - first]
                        sums[i] = sums[i] + piece * other
                return tuple(sums)

            sums = (jnp.zeros((last - first, right - left), F32),) * outs
            if sources == group:
                sums = some_sources(0, sums)
            else:
                sums = lax.fori_loop(0, sources // group, some_sources, sums)
            for i in range(outs):
                sums_ref[i, first:last, left:right] = sums[i]

    degree = rank_ref[0] * degrees + lax.broadcasted_iota(jnp.int32, (degrees, slots), 0)
    alive = degree >= ids_ref[...]
    copies = []
    for i in range(outs):
        value = sums_ref[i]
        folded = value[:, :slots]
        for lat in range(1, lats):
            folded = folded + value[:, lat * slots : (lat + 1) * slots]
        done_ref[i] = jnp.where(alive, folded, 0.0).T
        copies.append(pltpu.make_async_copy(done_ref.at[i], out_ref.at[i], sems.at[i]))
        copies[-1].start()
    for copy in copies:
        copy.wait()


def local(n_lat, n_wave, spectra, legendre, wave_m, nlon, coriolis, gauss_quadrature_weight):
    lats, slots, total = legendre.shape
    fields, levels = spectra.shape[:2]
    waves = wave_m.shape[0]
    degrees = spectra.shape[4]
    columns = lats * slots
    owned = lats * levels // n_wave
    lat_rank = lax.axis_index("lat").reshape(1)
    wave_rank = lax.axis_index("wave").reshape(1)
    steps = -(-(NLON // 4 + 1) // BASE)

    turned = call(
        turn_kernel,
        "turn",
        jax.ShapeDtypeStruct((total, columns), BF16),
        [ANY],
        [pltpu.VMEM((columns, total), BF16), pltpu.SemaphoreType.DMA((-(-total // LANES),))],
        bytes_accessed=4 * total * columns,
    )(legendre.reshape(columns, total))
    turned = lax.all_to_all(turned.reshape(n_lat, degrees, columns), "lat", 0, 0, tiled=True)

    own_ids = lax.dynamic_slice_in_dim(wave_m, wave_rank[0] * slots, slots, 0).reshape(1, slots)
    all_ids = wave_m.reshape(1, waves)
    spectra_turned = call(
        functools.partial(turn_spectra_kernel, lats, fields),
        "turn_spectra",
        jax.ShapeDtypeStruct((2 * fields * levels, degrees, columns), F32),
        [SMEM, VMEM, VMEM],
        flops=10 * fields * levels * degrees * columns,
        bytes_accessed=8 * fields * levels * degrees * columns,
    )(lat_rank, spectra.reshape(2 * fields * levels, slots, degrees), own_ids)

    table = call(
        functools.partial(table_kernel, levels),
        "table",
        jax.ShapeDtypeStruct((owned, steps * BASE, 2 * waves), BF16),
        [SMEM, SMEM, VMEM],
        [pltpu.VMEM((2, BASE, waves), F32), pltpu.VMEM((2, steps, waves), F32)],
        flops=16 * owned * steps * BASE * waves,
        bytes_accessed=4 * owned * steps * BASE * waves,
    )(wave_rank, nlon, all_ids)

    partial = call(
        functools.partial(forward_kernel, levels, owned),
        "forward",
        jax.ShapeDtypeStruct((n_lat * n_wave, owned, 2 * fields, slots), BF16),
        [VMEM, VMEM],
        flops=4 * n_lat * fields * levels * degrees * columns,
        bytes_accessed=8 * fields * levels * degrees * columns,
    )(turned, spectra_turned)
    partial = lax.all_to_all(partial, ("lat", "wave"), 0, 0, tiled=True)

    back = call(
        functools.partial(grid_kernel, levels),
        "grid",
        jax.ShapeDtypeStruct((n_lat * n_wave, owned, 4, slots), BF16),
        [SMEM, SMEM, SMEM, SMEM, VMEM, VMEM, VMEM],
        [pltpu.VMEM((24, 2 * waves), F32)],
        flops=128 * owned * steps * BASE * waves,
        bytes_accessed=4 * owned * steps * BASE * waves,
    )(wave_rank, nlon, coriolis, gauss_quadrature_weight, partial, table, all_ids)
    back = lax.all_to_all(back, ("lat", "wave"), 0, 0, tiled=True)

    outs = 4 * levels
    out = call(
        functools.partial(backward_kernel, levels),
        "backward",
        jax.ShapeDtypeStruct((outs, slots, degrees), F32),
        [SMEM, VMEM, VMEM, VMEM],
        [
            pltpu.VMEM((n_lat, outs, 8, columns), F32),
            pltpu.VMEM((outs, degrees, columns), F32),
            pltpu.VMEM((outs, slots, degrees), F32),
            pltpu.SemaphoreType.DMA((outs,)),
        ],
        out_specs=ANY,
        flops=2 * n_lat * outs * degrees * columns,
        bytes_accessed=8 * outs * degrees * slots,
    )(lat_rank, turned, back, own_ids)
    return out.reshape(2, levels, 2, slots, degrees)


def solution(mesh):
    placed = (
        P(None, None, None, "wave", "lat"),
        P("lat", "wave", None),
        P(),
        P("lat"),
        P("lat"),
        P("lat"),
    )
    return jax.shard_map(
        functools.partial(local, mesh.shape["lat"], mesh.shape["wave"]),
        mesh=mesh,
        in_specs=placed,
        out_specs=P(None, None, None, "wave", "lat"),
        check_vma=False,
    )
```

time: 64.9 us -> 52.9 us (0.82)
  Pallas kernels: 16.2 us -> 9.2 us
  local copies, waits for them, and re-layouts: 7.09 us -> 1.85 us
    pallas_call x5 -> x6, Pallas kernels: 16.2 us -> 9.2 us  [the longest x1 2.22 us: local(): call(functools.partial(grid_kernel, levels), 'grid', jax.ShapeDtypeStruct...]
    reshape x5 -> x1, local copies, waits for them, and re-layouts: 2.31 us -> 0.01 us  [local(): all_ids = wave_m.reshape(1, waves)]
    convert_element_type x5 -> x0, local copies, waits for them, and re-layouts: 1.6 us -> none  [the longest x3 0.91 us: local(): back = back.reshape(n_lat, 4 * levels, columns).astype(F32)]
    all_to_all x1, waiting for transfers between devices: 14 us -> 15.5 us  [local(): lax.all_to_all(turned.reshape(n_lat, degrees, columns), 'lat', 0, 0, tile...]
    all_to_all x1, waiting for transfers between devices: 7.77 us -> 6.85 us  [local(): partial = lax.all_to_all(partial, ('lat', 'wave'), 0, 0, tiled=True)]
    pallas_call x1 -> x0, local copies, waits for them, and re-layouts: 0.91 us -> none  [local(): pl.pallas_call(forward_kernel, out_shape=jax.ShapeDtypeStruct((n_lat, 6 *...]
where the time goes in v2:
time: 52.9 us; the launch traced here: 52.6 us
  waiting for transfers between devices  22.4 us (42%)
  starting transfers between devices  9.91 us (19%)
  Pallas kernels  9.2 us (17%)
  blocking collectives  9.18 us (17%)
  local copies, waits for them, and re-layouts  1.85 us (3%)
    all_to_all x1, waiting for transfers between devices, local(): lax.all_to_all(turned.reshape(n_lat, degrees, columns), 'lat', 0, 0, tile...  15.5 us
    all_to_all x1, blocking collectives, local(): back = lax.all_to_all(back, ('lat', 'wave'), 0, 0, tiled=True)  9.18 us
    all_to_all x1, waiting for transfers between devices, local(): partial = lax.all_to_all(partial, ('lat', 'wave'), 0, 0, tiled=True)  6.85 us
    all_to_all x1, starting transfers between devices, local(): lax.all_to_all(turned.reshape(n_lat, degrees, columns), 'lat', 0, 0, tile...  6.37 us
    all_to_all x1, starting transfers between devices, local(): partial = lax.all_to_all(partial, ('lat', 'wave'), 0, 0, tiled=True)  3.54 us
    pallas_call x1, Pallas kernels, local(): call(functools.partial(grid_kernel, levels), 'grid', jax.ShapeDtypeStruct...  2.22 us
    pallas_call x1, Pallas kernels, local(): call(functools.partial(forward_kernel, levels, owned), 'forward', jax.Sha...  1.88 us
    pallas_call x1, Pallas kernels, local(): call(functools.partial(backward_kernel, levels), 'backward', jax.ShapeDty...  1.68 us
  transfers between devices with their start and end apart: 2, of which 2 were waited for; matrix products, arithmetic and copies ran while one was open for 1% of the time, Pallas kernels for 4%

profile of v2, /device:TPU:0, one launch (start us, length us, event | category | flops | bytes accessed | tf_op | source)
XLA Modules:
  0.0 52.6 jit_solution(1456626638273585103)
XLA Ops:
  0.0 0.0 copy-start
  0.0 1.1 %copy-done = bf16[2,192,768]{2,1,0:T(8,128)(2,1)S(1)} copy-done((bf16[2,192,768]{2,1,0:T(8,128)(2,1)S(1)}, bf16[2,192,768]{2,1,0:T(8,128)(2,1)}, u32[]{:S(2)}) %copy-start) | copy-done | bytes 589848
  1.1 0.0 copy-start.1
  1.1 1.5 %turn.1 = bf16[768,384]{1,0:T(8,128)(2,1)} custom-call(bf16[384,768]{1,0:T(8,128)(2,1)S(1)} %bitcast.7), custom_call_target="tpu_custom_call" | custom-call | bytes 1179648 | tf_op jit(solution)/shard_map/turn/pallas_call | solution.py:317
  2.6 6.4 %all-to-all-start = ((bf16[8,96,384]{2,1,0:T(8,128)(2,1)}), bf16[8,96,384]{2,1,0:T(8,128)(2,1)S(1)}, u32[]{:S(2)}, u32[]{:S(2)}) async-start(bf16[8,96,384]{2,1,0:T(8,128)(2,1)} %bitcast.2), calls=%async_computation | async-start | bytes 1179648 | tf_op jit(solution)/shard_map/all_to_all | solution.py:325
  8.9 0.8 %dynamic_slice.3 = s32[192]{0:T(256)S(1)} dynamic-slice(s32[768]{0:T(1024)} %param.8, s32[]{:T(128)S(6)} %select_n.3), dynamic_slice_sizes={192} | dynamic-slice | bytes 1540 | tf_op jit(solution)/shard_map/dynamic_slice | solution.py:327
  9.7 0.0 copy-done.1
  9.7 0.0 copy-start.5
  9.7 0.0 copy-start.2
  9.7 0.4 turn_spectra.1.spectra_ref
  10.1 0.0 copy-start.3
  10.2 0.0 copy-start.4
  10.2 15.5 %all-to-all-done.legendre_ref = bf16[8,96,384]{2,1,0:T(8,128)(2,1)S(1)} async-done(((bf16[8,96,384]{2,1,0:T(8,128)(2,1)}), bf16[8,96,384]{2,1,0:T(8,128)(2,1)S(1)}, u32[]{:S(2)}, u32[]{:S(2)}) %all-to-all-start) | async-done | bytes 589856 | tf_op jit(solution)/shard_map/all_to_all | solution.py:325
  25.7 1.9 %forward.1 = bf16[32,1,6,192]{3,2,1,0:T(8,128)(2,1)} custom-call(bf16[8,96,384]{2,1,0:T(8,128)(2,1)S(1)} %all-to-all-done.legendre_ref, f32[12,96,384]{2,1,0:T(8,128)S(1)} %turn_spectra.1.spectra_ref), custom_call_target="tpu_custom_call" | custom-call | flops 7077888 | bytes 1769472 | tf_op jit(solution)/shard_map/forward/pallas_call | solution.py:348
  27.6 3.5 %all-to-all-start.1 = ((bf16[32,1,6,192]{3,2,1,0:T(8,128)(2,1)}), bf16[32,1,6,192]{3,2,1,0:T(8,128)(2,1)S(1)}, u32[]{:S(2)}, u32[]{:S(2)}) async-start(bf16[32,1,6,192]{3,2,1,0:T(8,128)(2,1)} %forward.1), calls=%async_computation.1 | async-start | bytes 262144 | tf_op jit(solution)/shard_map/all_to_all | solution.py:356
  31.1 0.0 copy-done.5
  31.1 0.0 copy-done.2
  31.1 1.5 %table.1.table_ref = bf16[1,800,1536]{2,1,0:T(8,128)(2,1)S(1)} custom-call(s32[1]{0:T(128)} %bitcast.3.rank_ref, s32[2]{0:T(128)S(1)} %copy-done.2, s32[1,768]{1,0:T(1,128)S(1)} %reshape.30.ids_ref), custom_call_target="tpu_custom_call" | custom-call | flops 9830400 | bytes 2457600 | tf_op jit(solution)/shard_map/table/pallas_call | solution.py:338
  32.6 6.9 %all-to-all-done.1.partial_ref = bf16[32,1,6,192]{3,2,1,0:T(8,128)(2,1)S(1)} async-done(((bf16[32,1,6,192]{3,2,1,0:T(8,128)(2,1)}), bf16[32,1,6,192]{3,2,1,0:T(8,128)(2,1)S(1)}, u32[]{:S(2)}, u32[]{:S(2)}) %all-to-all-start.1) | async-done | bytes 73760 | tf_op jit(solution)/shard_map/all_to_all | solution.py:356
  39.5 0.0 copy-done.3
  39.5 0.0 copy-done.4
  39.5 2.2 %grid.1 = bf16[32,1,4,192]{3,2,1,0:T(4,128)(2,1)S(1)} custom-call(s32[1]{0:T(128)} %bitcast.3.rank_ref, s32[2]{0:T(128)S(1)} %copy-done.2, f32[2]{0:T(128)S(1)} %copy-done.3, f32[2]{0:T(128)S(1)} %copy-done.4, bf16[32,1,6,192]{3,2,1,0:T(8,128)(2,1)S(1)} %all-to-all-done.1.partial_ref, bf16[1,800,1536]{2,1,0:T(8,128)(2,1)S(1)} %table.1.table_ref, ...), custom_call_target="tpu_custom_call" | custom-call | flops 78643200 | bytes 2457600 | tf_op jit(solution)/shard_map/grid/pallas_call | solution.py:358
  41.7 9.2 %all_to_all.15.back_ref = bf16[32,1,4,192]{3,2,1,0:T(4,128)(2,1)S(1)} all-to-all(bf16[32,1,4,192]{3,2,1,0:T(4,128)(2,1)S(1)} %grid.1), channel_id=1, replica_groups=mesh['lat'=8,'wave'=4] {'lat','wave'}, dimensions={0} | all-to-all | bytes 98304 | tf_op jit(solution)/shard_map/all_to_all | solution.py:367
  50.9 1.7 %backward.1 = f32[8,192,96]{2,1,0:T(8,128)} custom-call(s32[1]{0:T(128)} %bitcast.rank_ref, bf16[8,96,384]{2,1,0:T(8,128)(2,1)S(1)} %all-to-all-done.legendre_ref, bf16[32,1,4,192]{3,2,1,0:T(4,128)(2,1)S(1)} %all_to_all.15.back_ref, s32[1,192]{1,0:T(1,128)S(1)} %bitcast.10), custom_call_target="tpu_custom_call" | custom-call | flops 4718592 | bytes 1179648 | tf_op jit(solution)/shard_map/backward/pallas_call | solution.py:370
  (1 shorter events, 0.0 us)
Async XLA Ops:
  0.0 1.1 %copy-start = (bf16[2,192,768]{2,1,0:T(8,128)(2,1)S(1)}, bf16[2,192,768]{2,1,0:T(8,128)(2,1)}, u32[]{:S(2)}) copy-start(bf16[2,192,768]{2,1,0:T(8,128)(2,1)} %param.7) | copy-start | bytes 1769476
  1.1 8.6 %copy-start.1 = (bf16[3,2,2,192,96]{4,3,2,1,0:T(8,128)(2,1)S(1)}, bf16[3,2,2,192,96]{4,3,2,1,0:T(8,128)(2,1)}, u32[]{:S(2)}) copy-start(bf16[3,2,2,192,96]{4,3,2,1,0:T(8,128)(2,1)} %param.6) | copy-start | bytes 1327108
  2.6 23.1 %all-to-all-start = ((bf16[8,96,384]{2,1,0:T(8,128)(2,1)}), bf16[8,96,384]{2,1,0:T(8,128)(2,1)S(1)}, u32[]{:S(2)}, u32[]{:S(2)}) async-start(bf16[8,96,384]{2,1,0:T(8,128)(2,1)} %bitcast.2), calls=%async_computation | async-start | bytes 1179648 | tf_op jit(solution)/shard_map/all_to_all | solution.py:325
  9.7 21.4 %copy-start.5 = (s32[768]{0:T(1024)S(1)}, s32[768]{0:T(1024)}, u32[]{:S(2)}) copy-start(s32[768]{0:T(1024)} %param.8) | copy-start | bytes 9220
  9.7 21.4 %copy-start.2 = (s32[2]{0:T(128)S(1)}, s32[2]{0:T(128)}, u32[]{:S(2)}) copy-start(s32[2]{0:T(128)} %nlon_ref.3) | copy-start | bytes 28
  10.1 29.3 %copy-start.3 = (f32[2]{0:T(128)S(1)}, f32[2]{0:T(128)}, u32[]{:S(2)}) copy-start(f32[2]{0:T(128)} %coriolis_ref.1) | copy-start | bytes 28
  10.2 29.3 %copy-start.4 = (f32[2]{0:T(128)S(1)}, f32[2]{0:T(128)}, u32[]{:S(2)}) copy-start(f32[2]{0:T(128)} %weight_ref.1) | copy-start | bytes 28
  27.6 11.9 %all-to-all-start.1 = ((bf16[32,1,6,192]{3,2,1,0:T(8,128)(2,1)}), bf16[32,1,6,192]{3,2,1,0:T(8,128)(2,1)S(1)}, u32[]{:S(2)}, u32[]{:S(2)}) async-start(bf16[32,1,6,192]{3,2,1,0:T(8,128)(2,1)} %forward.1), calls=%async_computation.1 | async-start | bytes 262144 | tf_op jit(solution)/shard_map/all_to_all | solution.py:356

commit v3 on v2

v3 whole, which is shorter than its diff:
```python
import functools
import math

import jax
import jax.numpy as jnp
from jax import lax
from jax.experimental import pallas as pl
from jax.experimental.pallas import tpu as pltpu
from jax.sharding import PartitionSpec as P

NLON = 3088
BASE = 16
LANES = 128

F32 = jnp.float32
BF16 = jnp.bfloat16

VMEM = pl.BlockSpec(memory_space=pltpu.VMEM)
SMEM = pl.BlockSpec(memory_space=pltpu.SMEM)
HBM = pl.BlockSpec(memory_space=pltpu.HBM)


def call(
    body, name, out_shape, in_specs, scratch=(), out_specs=VMEM, flops=0, bytes_accessed=0,
    grant=16 * 1024 * 1024,
):
    return pl.pallas_call(
        body,
        out_shape=out_shape,
        in_specs=in_specs,
        out_specs=out_specs,
        scratch_shapes=scratch,
        name=name,
        cost_estimate=pl.CostEstimate(
            flops=flops, bytes_accessed=bytes_accessed, transcendentals=0
        ),
        compiler_params=pltpu.CompilerParams(vmem_limit_bytes=grant),
    )


def pieces(extent, size):
    return [(first, min(first + size, extent)) for first in range(0, extent, size)]


def message_shape(rows, slots):
    if slots > LANES and slots % LANES == LANES // 2 and rows % 2 == 0:
        lines = rows * (slots // LANES) + rows // 2
        return (-(-lines // 2), 2, LANES)
    return (rows, slots)


def put_message(ref, index, value):
    if len(ref.shape) == len(index) + 2:
        ref[index] = value.astype(BF16)
        return
    rows, slots = value.shape
    lines = [value[:, first : first + LANES] for first in range(0, slots - LANES + 1, LANES)]
    rest = value[:, slots - LANES // 2 :]
    lines.append(jnp.concatenate([rest[: rows // 2], rest[rows // 2 :]], axis=1))
    if lines[-1].shape[0] % 2:
        lines.append(lines[-1][:1])
    lines = jnp.concatenate(lines, axis=0)
    for k in range(lines.shape[0] // 2):
        ref[index + (k,)] = lines[2 * k : 2 * k + 2].astype(BF16)


def get_message(message, rows, slots):
    if message.ndim == 2:
        return message
    lines = jnp.concatenate([message[k] for k in range(message.shape[0])], axis=0)
    whole = slots // LANES
    parts = [lines[k * rows : (k + 1) * rows] for k in range(whole)]
    rest = lines[whole * rows : whole * rows + rows // 2]
    half = LANES // 2
    parts.append(jnp.concatenate([rest[:, :half], rest[:, half:]], axis=0))
    return jnp.concatenate(parts, axis=1)


def turn_kernel(begin, legendre_ref, out_ref, held_ref, turned_ref, sems):
    width = out_ref.shape[1]
    parts = pieces(legendre_ref.shape[1], 2 * LANES)
    arrivals, departures = [], []
    for i, (first, last) in enumerate(parts):
        arrivals.append(
            pltpu.make_async_copy(
                legendre_ref.at[begin : begin + width, first:last],
                held_ref.at[:, first:last],
                sems.at[0, i],
            )
        )
        arrivals[-1].start()
    for i, (first, last) in enumerate(parts):
        arrivals[i].wait()
        turned_ref[first:last, :] = held_ref[:, first:last].T
        departures.append(
            pltpu.make_async_copy(turned_ref.at[first:last], out_ref.at[first:last], sems.at[1, i])
        )
        departures[-1].start()
    for copy in departures:
        copy.wait()


def turn_spectra_kernel(repeats, fields, rank_ref, spectra_ref, ids_ref, out_ref):
    count, slots, degrees = spectra_ref.shape
    levels = count // (2 * fields)
    degree = rank_ref[0] * degrees + lax.broadcasted_iota(jnp.int32, (degrees, slots), 0)
    alive = degree >= ids_ref[...]
    for i in range(count):
        field, level, part = i // (2 * levels), (i // 2) % levels, i % 2
        turned = jnp.where(alive, spectra_ref[i].astype(F32).T, 0.0)
        place = (level * fields + field) * 2 + part
        out_ref[place] = jnp.concatenate([turned] * repeats, axis=1)


def forward_sums(begin, g, group, legendre_ref, spectra_ref):
    degrees, width = legendre_ref.shape[1:]
    fields = spectra_ref.shape[0]
    tiles = [[] for _ in range(group)]
    for left, right in pieces(width, LANES):
        sums = [[None] * fields for _ in range(group)]
        for first, last in pieces(degrees, 16):
            own = [
                legendre_ref[g * group + k, first:last, left:right].astype(F32)
                for k in range(group)
            ]
            for i in range(fields):
                other = spectra_ref[i, first:last, begin + left : begin + right]
                for k in range(group):
                    product = own[k] * other
                    if last - first == 16:
                        product = product[:8] + product[8:]
                    else:
                        product = jnp.sum(product, axis=0, keepdims=True)
                    sums[k][i] = product if sums[k][i] is None else sums[k][i] + product
        for k in range(group):
            rows = [jnp.sum(value, axis=0, keepdims=True) for value in sums[k]]
            tiles[k].append(jnp.concatenate(rows, axis=0))
    return [jnp.concatenate(tile, axis=1) for tile in tiles]


def early_forward_kernel(begin, legendre_ref, spectra_ref, out_ref):
    sources = legendre_ref.shape[0]
    group = 2 if sources % 2 == 0 else 1

    def some_sources(g, carry):
        for k, value in enumerate(forward_sums(begin, g, group, legendre_ref, spectra_ref)):
            out_ref[g * group + k] = value
        return carry

    lax.fori_loop(0, sources // group, some_sources, 0)


def last_forward_kernel(begin, levels, owned, slots, legendre_ref, spectra_ref, *refs):
    *early_refs, out_ref = refs
    sources = legendre_ref.shape[0]
    fields = spectra_ref.shape[0]
    columns = spectra_ref.shape[2]
    per_level = fields // levels
    lats = columns // slots
    targets = out_ref.shape[0] // sources
    group = 2 if sources % 2 == 0 else 1

    def some_sources(g, carry):
        for k, value in enumerate(forward_sums(begin, g, group, legendre_ref, spectra_ref)):
            a = g * group + k
            value = jnp.concatenate([ref[a] for ref in early_refs] + [value], axis=1)
            for row in range(lats * levels):
                lat, level = row // levels, row % levels
                message = value[
                    level * per_level : (level + 1) * per_level,
                    lat * slots : (lat + 1) * slots,
                ]
                put_message(out_ref, (a * targets + row // owned, row % owned), message)
        return carry

    lax.fori_loop(0, sources // group, some_sources, 0)


def cos_sin(places, ids, count, inverse):
    quads = 4.0 * places * ids
    turns = jnp.floor(quads * inverse + 0.5)
    angle = (quads - turns * count) * (inverse * (math.pi / 2))
    square = angle * angle
    c = 1.0 + square * (-1 / 2 + square * (1 / 24 + square * (-1 / 720 + square * (1 / 40320))))
    s = angle * (
        1.0 + square * (-1 / 6 + square * (1 / 120 + square * (-1 / 5040 + square * (1 / 362880))))
    )
    quadrant = turns - 4.0 * jnp.floor(turns * 0.25)
    odd = (quadrant == 1.0) | (quadrant == 3.0)
    cosine = jnp.where(odd, s, c)
    sine = jnp.where(odd, c, s)
    cosine = jnp.where((quadrant == 1.0) | (quadrant == 2.0), -cosine, cosine)
    sine = jnp.where(quadrant >= 2.0, -sine, sine)
    return cosine, sine


def image_signs(ids):
    quadrant = ids - 4.0 * jnp.floor(ids * 0.25)
    one = jnp.ones_like(ids)
    none = jnp.zeros_like(ids)
    parity = jnp.where((quadrant == 1.0) | (quadrant == 3.0), -1.0, 1.0)
    c = jnp.where(quadrant == 0.0, 1.0, jnp.where(quadrant == 2.0, -1.0, 0.0))
    s = jnp.where(quadrant == 1.0, 1.0, jnp.where(quadrant == 3.0, -1.0, 0.0))
    cos_cos = [one, one, parity, parity, c, c, c, c]
    cos_sin = [none, none, none, none, s, -s, -s, s]
    sin_cos = [none, none, none, none, s, s, -s, -s]
    sin_sin = [one, -one, -parity, parity, -c, c, -c, c]
    return [jnp.concatenate(rows, axis=0) for rows in (cos_cos, cos_sin, sin_cos, sin_sin)]


def table_kernel(
    levels, rank_ref, nlon_ref, coriolis_ref, weight_ref, ids_ref,
    table_ref, left_ref, right_ref, share_ref, rotation_ref, base_ref, step_ref,
):
    owned = table_ref.shape[0]
    steps = step_ref.shape[1]
    waves = ids_ref.shape[1]
    ids = ids_ref[...].astype(F32)
    signs = image_signs(ids)
    for offset in range(owned):
        latitude = (rank_ref[0] * owned + offset) // levels
        count_int = nlon_ref[latitude]
        count = jnp.full((1, waves), count_int.astype(F32))
        inverse = 1.0 / count
        rows = lax.broadcasted_iota(jnp.int32, (BASE, waves), 0).astype(F32)
        base_ref[0], base_ref[1] = cos_sin(rows, ids, count, inverse)
        rows = lax.broadcasted_iota(jnp.int32, (steps, waves), 0).astype(F32) * BASE
        step_ref[0], step_ref[1] = cos_sin(rows, ids, count, inverse)
        for a in range(steps):
            step_c = step_ref[0, a : a + 1, :]
            step_s = step_ref[1, a : a + 1, :]
            base_c = base_ref[0]
            base_s = base_ref[1]
            here = slice(a * BASE, (a + 1) * BASE)
            table_ref[offset, here, :waves] = (step_c * base_c - step_s * base_s).astype(BF16)
            table_ref[offset, here, waves:] = (step_s * base_c + step_c * base_s).astype(BF16)

        factor = jnp.where(ids == 0.0, 1.0, 2.0)
        factor = jnp.where(2.0 * ids < count, factor, 0.0)
        scale = jnp.where(factor > 0.0, weight_ref[latitude] / count, 0.0)
        left_ref[offset, 0] = signs[0] * factor
        left_ref[offset, 1] = -signs[2] * factor
        left_ref[offset, 2] = signs[1] * factor
        left_ref[offset, 3] = -signs[3] * factor
        right_ref[offset, 0] = signs[0] * scale
        right_ref[offset, 1] = signs[1] * scale
        right_ref[offset, 2] = -signs[2] * scale
        right_ref[offset, 3] = -signs[3] * scale
        place = lax.broadcasted_iota(jnp.int32, share_ref.shape[1:], 1)
        share = jnp.where((place == 0) | (8 * place == count_int), 0.5, 1.0)
        share_ref[offset] = jnp.where(8 * place <= count_int, share, 0.0)
        rotation_ref[offset] = jnp.full(rotation_ref.shape[1:], coriolis_ref[latitude])


def grid_kernel(
    slots, partial_ref, table_ref, left_ref, right_ref, share_ref, rotation_ref, out_ref, rows_ref
):
    owned = partial_ref.shape[1]
    waves = left_ref.shape[-1]
    parts = waves // slots
    sources = partial_ref.shape[0] // parts
    for offset in range(owned):

        def total(w):
            def add(a, value):
                return value + partial_ref[a * parts + w, offset].astype(F32)

            if sources > 8:
                return lax.fori_loop(1, sources, add, partial_ref[w, offset].astype(F32))
            value = partial_ref[w, offset].astype(F32)
            for a in range(1, sources):
                value = add(a, value)
            return value

        fourier = jnp.concatenate(
            [get_message(total(w), 6, slots) for w in range(parts)], axis=1
        )
        fourier = fourier.astype(BF16).astype(F32)
        for field in range(3):
            here = slice(8 * field, 8 * field + 8)
            real = fourier[2 * field : 2 * field + 1]
            imag = fourier[2 * field + 1 : 2 * field + 2]
            rows_ref[here, :waves] = real * left_ref[offset, 0] + imag * left_ref[offset, 1]
            rows_ref[here, waves:] = real * left_ref[offset, 2] + imag * left_ref[offset, 3]
        grid = lax.dot_general(
            rows_ref[...].astype(BF16),
            table_ref[offset],
            (((1,), (1,)), ((), ())),
            preferred_element_type=F32,
        )
        vorticity, divergence, temperature = grid[0:8], grid[8:16], grid[16:24]
        share = share_ref[offset]

        def shared(product):
            rounded = jnp.where(share > 0.0, product, 0.0).astype(BF16)
            return rounded.astype(F32) * share

        stretch = shared(-(vorticity + rotation_ref[offset]) * divergence)
        heating = shared(-temperature * divergence)
        products = jnp.concatenate([stretch, heating], axis=0).astype(BF16)
        sums = jnp.dot(products, table_ref[offset], preferred_element_type=F32)
        both = []
        for q in range(2):
            c = sums[8 * q : 8 * q + 8, :waves]
            s = sums[8 * q : 8 * q + 8, waves:]
            for k in range(2):
                term = c * right_ref[offset, 2 * k] + s * right_ref[offset, 2 * k + 1]
                both.append(jnp.sum(term, axis=0, keepdims=True))
        back = jnp.concatenate(both, axis=0)
        for w in range(parts):
            part = back[:, w * slots : (w + 1) * slots]

            def put(a, carry):
                put_message(out_ref, (a * parts + w, offset), part)
                return carry

            if sources > 8:
                lax.fori_loop(0, sources, put, 0)
            else:
                for a in range(sources):
                    put(a, 0)


def backward_kernel(
    levels, rank_ref, back_ref, ids_ref, *refs
):
    *legendre_refs, out_ref, wide_ref, sums_ref, done_ref, sems = refs
    sources, degrees = legendre_refs[0].shape[:2]
    columns = wide_ref.shape[3]
    outs, slots, _ = out_ref.shape
    lats = columns // slots
    owned = back_ref.shape[1]
    targets = back_ref.shape[0] // sources
    group = min(sources, 8)

    def spread(a, carry):
        for level in range(levels):
            rows = []
            for lat in range(lats):
                row = lat * levels + level
                message = back_ref[a * targets + row // owned, row % owned].astype(F32)
                rows.append(get_message(message, 4, slots))
            both = jnp.concatenate(rows, axis=1)
            for i in range(4):
                place = ((i // 2) * levels + level) * 2 + i % 2
                wide_ref[a, place] = jnp.broadcast_to(both[i : i + 1], (8, columns))
        return carry

    if sources > 8:
        lax.fori_loop(0, sources, spread, 0)
    else:
        for a in range(sources):
            spread(a, 0)

    degree = rank_ref[0] * degrees + lax.broadcasted_iota(jnp.int32, (degrees, slots), 0)
    alive = degree >= ids_ref[...]
    tiles = []
    begin = 0
    for legendre_ref in legendre_refs:
        width = legendre_ref.shape[2]
        tiles += [(legendre_ref, begin, *piece) for piece in pieces(width, LANES)]
        begin += width
    copies = []
    for own in pieces(outs, 4):
        for first, last in pieces(degrees, 16):
            for legendre_ref, begin, left, right in tiles:
                whole = slice(begin + left, begin + right)

                def some_sources(g, sums):
                    sums = list(sums)
                    for k in range(group):
                        piece = legendre_ref[g * group + k, first:last, left:right].astype(F32)
                        for i in range(*own):
                            other = wide_ref[g * group + k, i, :, whole]
                            other = jnp.concatenate([other, other], axis=0)[: last - first]
                            term = piece * other
                            past = sums[i - own[0]]
                            sums[i - own[0]] = term if past is None else past + term
                    return tuple(sums)

                if sources == group:
                    sums = some_sources(0, (None,) * (own[1] - own[0]))
                else:
                    zero = jnp.zeros((last - first, right - left), F32)
                    sums = (zero,) * (own[1] - own[0])
                    sums = lax.fori_loop(0, sources // group, some_sources, sums)
                for i in range(*own):
                    sums_ref[i, first:last, whole] = sums[i - own[0]]
        for i in range(*own):
            value = sums_ref[i]
            folded = value[:, :slots]
            for lat in range(1, lats):
                folded = folded + value[:, lat * slots : (lat + 1) * slots]
            done_ref[i] = jnp.where(alive, folded, 0.0).T
            copies.append(pltpu.make_async_copy(done_ref.at[i], out_ref.at[i], sems.at[i]))
            copies[-1].start()
    for copy in copies:
        copy.wait()


def local(n_lat, n_wave, spectra, legendre, wave_m, nlon, coriolis, gauss_quadrature_weight):
    lats, slots, total = legendre.shape
    fields, levels = spectra.shape[:2]
    waves = wave_m.shape[0]
    degrees = spectra.shape[4]
    columns = lats * slots
    owned = lats * levels // n_wave
    lat_rank = lax.axis_index("lat").reshape(1)
    wave_rank = lax.axis_index("wave").reshape(1)
    steps = -(-(NLON // 8 + 1) // BASE)
    places = steps * BASE

    chunks = [(0, columns)]
    turned = []
    for begin, end in chunks:
        width = end - begin
        chunk = call(
            functools.partial(turn_kernel, begin),
            "turn",
            jax.ShapeDtypeStruct((total, width), BF16),
            [HBM],
            [
                pltpu.VMEM((width, total), BF16),
                pltpu.VMEM((total, width), BF16),
                pltpu.SemaphoreType.DMA((2, -(-total // (2 * LANES)))),
            ],
            out_specs=HBM,
            bytes_accessed=4 * total * width,
            grant=None,
        )(legendre.reshape(columns, total))
        chunk = chunk.reshape(n_lat, degrees, width)
        turned.append(lax.all_to_all(chunk, "lat", 0, 0, tiled=True))

    own_ids = lax.dynamic_slice_in_dim(wave_m, wave_rank[0] * slots, slots, 0).reshape(1, slots)
    all_ids = wave_m.reshape(1, waves)
    spectra_turned = call(
        functools.partial(turn_spectra_kernel, lats, fields),
        "turn_spectra",
        jax.ShapeDtypeStruct((2 * fields * levels, degrees, columns), F32),
        [SMEM, VMEM, VMEM],
        flops=10 * fields * levels * degrees * columns,
        bytes_accessed=8 * fields * levels * degrees * columns,
    )(lat_rank, spectra.reshape(2 * fields * levels, slots, degrees), own_ids)

    row = call(
        functools.partial(table_kernel, levels),
        "table",
        (
            jax.ShapeDtypeStruct((owned, places, 2 * waves), BF16),
            jax.ShapeDtypeStruct((owned, 4, 8, waves), F32),
            jax.ShapeDtypeStruct((owned, 4, 8, waves), F32),
            jax.ShapeDtypeStruct((owned, 8, places), F32),
            jax.ShapeDtypeStruct((owned, 8, places), F32),
        ),
        [SMEM, SMEM, SMEM, SMEM, VMEM],
        [pltpu.VMEM((2, BASE, waves), F32), pltpu.VMEM((2, steps, waves), F32)],
        out_specs=(VMEM,) * 5,
        flops=16 * owned * places * waves,
        bytes_accessed=4 * owned * places * waves,
    )(wave_rank, nlon, coriolis, gauss_quadrature_weight, all_ids)
    spectra_turned, *row = lax.optimization_barrier((spectra_turned, *row))

    early = []
    for (begin, end), chunk in zip(chunks[:-1], turned[:-1]):
        early.append(
            call(
                functools.partial(early_forward_kernel, begin),
                "early_forward",
                jax.ShapeDtypeStruct((n_lat, 2 * fields * levels, end - begin), F32),
                [VMEM, VMEM],
                flops=4 * n_lat * fields * levels * degrees * (end - begin),
                bytes_accessed=8 * fields * levels * degrees * (end - begin),
            )(chunk, spectra_turned)
        )
    begin, end = chunks[-1]
    partial = call(
        functools.partial(last_forward_kernel, begin, levels, owned, slots),
        "forward",
        jax.ShapeDtypeStruct((n_lat * n_wave, owned) + message_shape(2 * fields, slots), BF16),
        [VMEM, VMEM] + [VMEM] * len(early),
        flops=4 * n_lat * fields * levels * degrees * (end - begin),
        bytes_accessed=8 * fields * levels * degrees * (end - begin),
    )(turned[-1], spectra_turned, *early)
    partial = lax.all_to_all(partial, ("lat", "wave"), 0, 0, tiled=True)

    back = call(
        functools.partial(grid_kernel, slots),
        "grid",
        jax.ShapeDtypeStruct((n_lat * n_wave, owned, 4, slots), BF16),
        [VMEM] * 6,
        [pltpu.VMEM((24, 2 * waves), F32)],
        flops=128 * owned * places * waves,
        bytes_accessed=4 * owned * places * waves,
    )(partial, *row)
    back = lax.all_to_all(back, ("lat", "wave"), 0, 0, tiled=True)

    outs = 4 * levels
    out = call(
        functools.partial(backward_kernel, levels),
        "backward",
        jax.ShapeDtypeStruct((outs, slots, degrees), F32),
        [SMEM, VMEM, VMEM] + [VMEM] * len(turned),
        [
            pltpu.VMEM((n_lat, outs, 8, columns), F32),
            pltpu.VMEM((outs, degrees, columns), F32),
            pltpu.VMEM((outs, slots, degrees), F32),
            pltpu.SemaphoreType.DMA((outs,)),
        ],
        out_specs=HBM,
        flops=2 * n_lat * outs * degrees * columns,
        bytes_accessed=8 * outs * degrees * slots,
    )(lat_rank, back, own_ids, *turned)
    return out.reshape(2, levels, 2, slots, degrees)


def solution(mesh):
    placed = (
        P(None, None, None, "wave", "lat"),
        P("lat", "wave", None),
        P(),
        P("lat"),
        P("lat"),
        P("lat"),
    )
    return jax.shard_map(
        functools.partial(local, mesh.shape["lat"], mesh.shape["wave"]),
        mesh=mesh,
        in_specs=placed,
        out_specs=P(None, None, None, "wave", "lat"),
        check_vma=False,
    )
```

time: 52.9 us -> 50 us (0.945)
  blocking collectives: 9.18 us -> 20.2 us
  waiting for transfers between devices: 22.4 us -> 13.9 us
  starting transfers between devices: 9.91 us -> 6.5 us
  Pallas kernels: 9.2 us -> 7.83 us
  local copies, waits for them, and re-layouts: 1.85 us -> 1.15 us
    all_to_all x0 -> x1, blocking collectives: none -> 11 us  [local(): partial = lax.all_to_all(partial, ('lat', 'wave'), 0, 0, tiled=True)]
    all_to_all x2 -> x1, waiting for transfers between devices: 22.4 us -> 13.9 us  [local(): turned.append(lax.all_to_all(chunk, 'lat', 0, 0, tiled=True))]
    all_to_all x2 -> x1, starting transfers between devices: 9.91 us -> 6.5 us  [local(): turned.append(lax.all_to_all(chunk, 'lat', 0, 0, tiled=True))]
    pallas_call x4, Pallas kernels: 7.09 us -> 5.69 us  [the longest x1 2.03 us: local(): call(functools.partial(turn_kernel, begin), 'turn', jax.ShapeDtypeStruct(...]
    dynamic_slice x1, local copies, waits for them, and re-layouts: 0.76 us -> 0.08 us  [local(): lax.dynamic_slice_in_dim(wave_m, wave_rank[0] * slots, slots, 0)]
    unnamed x12 -> x14, local copies, waits for them, and re-layouts: 1.09 us -> 1.07 us
  transfers between devices with their start and end apart: 2 -> 1, of which waited for: 2 -> 1; matrix products, arithmetic and copies ran while one was open for 1% -> 0% of each run, Pallas kernels for 4% -> 3%
where the time goes in v3:
time: 50 us; the launch traced here: 49.7 us
  blocking collectives  20.2 us (40%)
  waiting for transfers between devices  13.9 us (28%)
  Pallas kernels  7.83 us (16%)
  starting transfers between devices  6.5 us (13%)
  local copies, waits for them, and re-layouts  1.15 us (2%)
    all_to_all x1, waiting for transfers between devices, local(): turned.append(lax.all_to_all(chunk, 'lat', 0, 0, tiled=True))  13.9 us
    all_to_all x1, blocking collectives, local(): partial = lax.all_to_all(partial, ('lat', 'wave'), 0, 0, tiled=True)  11 us
    all_to_all x1, blocking collectives, local(): back = lax.all_to_all(back, ('lat', 'wave'), 0, 0, tiled=True)  9.18 us
    all_to_all x1, starting transfers between devices, local(): turned.append(lax.all_to_all(chunk, 'lat', 0, 0, tiled=True))  6.5 us
    pallas_call x1, Pallas kernels, local(): call(functools.partial(turn_kernel, begin), 'turn', jax.ShapeDtypeStruct(...  2.03 us
    pallas_call x1, Pallas kernels, local(): call(functools.partial(backward_kernel, levels), 'backward', jax.ShapeDty...  1.71 us
    pallas_call x1, Pallas kernels, local(): call(functools.partial(last_forward_kernel, begin, levels, owned, slots),...  1.47 us
    pallas_call x1, Pallas kernels, local(): call(functools.partial(table_kernel, levels), 'table', (jax.ShapeDtypeStr...  1.19 us
  transfers between devices with their start and end apart: 1, of which 1 were waited for; matrix products, arithmetic and copies ran while one was open for 0% of the time, Pallas kernels for 3%

profile of v3, /device:TPU:0, one launch (start us, length us, event | category | flops | bytes accessed | tf_op | source)
XLA Modules:
  0.0 49.7 jit_solution(18305513724791984994)
XLA Ops:
  0.0 0.0 copy-start.6
  0.0 0.0 copy-start.2
  0.0 2.0 %turn.1 = bf16[768,384]{1,0:T(8,128)(2,1)} custom-call(bf16[384,768]{1,0:T(8,128)(2,1)} %bitcast.11), custom_call_target="tpu_custom_call" | custom-call | bytes 1179648 | tf_op jit(solution)/shard_map/turn/pallas_call | solution.py:417
  2.0 0.0 copy-start.3
  2.1 0.0 copy-start.4
  2.1 0.0 copy-start.5
  2.1 6.5 %all-to-all-start = ((bf16[8,96,384]{2,1,0:T(8,128)(2,1)}), bf16[8,96,384]{2,1,0:T(8,128)(2,1)S(1)}, u32[]{:S(2)}, u32[]{:S(2)}) async-start(bf16[8,96,384]{2,1,0:T(8,128)(2,1)} %bitcast.10), calls=%async_computation | async-start | bytes 1179648 | tf_op jit(solution)/shard_map/all_to_all | solution.py:432
  8.6 0.0 copy-done.6
  8.6 0.1 dynamic_slice.3
  8.7 0.0 copy-done.2
  8.7 0.4 turn_spectra.1.spectra_ref
  9.1 0.0 copy-done.3
  9.1 0.0 copy-done.4
  9.1 0.0 copy-done.5
  9.1 1.2 %table.1 = (bf16[1,400,1536]{2,1,0:T(8,128)(2,1)S(1)}, f32[1,4,8,768]{3,2,1,0:T(8,128)S(1)}, f32[1,4,8,768]{3,2,1,0:T(8,128)S(1)}, f32[1,8,400]{2,1,0:T(8,128)S(1)}, f32[1,8,400]{2,1,0:T(8,128)S(1)}) custom-call(s32[1]{0:T(128)} %bitcast.5.rank_ref, s32[2]{0:T(128)S(1)} %copy-done.3, f32[2]{0:T(128)S(1)} %copy-done.4, f32[2]{0:T(128)S(1)} %copy-done.5, ...), custom_call_target="tpu_custom_call" | custom-call | flops 4915200 | bytes 1228800 | tf_op jit(solution)/shard_map/table/pallas_call | solution.py:445
  10.3 0.0 copy-start
  10.3 1.0 %copy-done = bf16[1,400,1536]{2,1,0:T(8,128)(2,1)} copy-done((bf16[1,400,1536]{2,1,0:T(8,128)(2,1)}, bf16[1,400,1536]{2,1,0:T(8,128)(2,1)S(1)}, u32[]{:S(2)}) %copy-start) | copy-done | bytes 1228824
  11.4 13.9 %all-to-all-done.legendre_ref.refs_0_ = bf16[8,96,384]{2,1,0:T(8,128)(2,1)S(1)} async-done(((bf16[8,96,384]{2,1,0:T(8,128)(2,1)}), bf16[8,96,384]{2,1,0:T(8,128)(2,1)S(1)}, u32[]{:S(2)}, u32[]{:S(2)}) %all-to-all-start) | async-done | bytes 589856 | tf_op jit(solution)/shard_map/all_to_all | solution.py:432
  25.3 0.0 copy-start.1
  25.3 1.5 %forward.1 = bf16[32,1,5,2,128]{4,3,2,1,0:T(2,128)(2,1)S(1)} custom-call(bf16[8,96,384]{2,1,0:T(8,128)(2,1)S(1)} %all-to-all-done.legendre_ref.refs_0_, f32[12,96,384]{2,1,0:T(8,128)S(1)} %turn_spectra.1.spectra_ref), custom_call_target="tpu_custom_call" | custom-call | flops 7077888 | bytes 1769472 | tf_op jit(solution)/shard_map/forward/pallas_call | solution.py:476
  26.8 11.0 %all_to_all.15.partial_ref = bf16[32,1,5,2,128]{4,3,2,1,0:T(2,128)(2,1)S(1)} all-to-all(bf16[32,1,5,2,128]{4,3,2,1,0:T(2,128)(2,1)S(1)} %forward.1), channel_id=1, replica_groups=mesh['lat'=8,'wave'=4] {'lat','wave'}, dimensions={0} | all-to-all | bytes 163840 | tf_op jit(solution)/shard_map/all_to_all | solution.py:484
  37.8 0.0 copy-done.1
  37.8 1.0 %grid.1 = bf16[32,1,4,192]{3,2,1,0:T(4,128)(2,1)S(1)} custom-call(bf16[32,1,5,2,128]{4,3,2,1,0:T(2,128)(2,1)S(1)} %all_to_all.15.partial_ref, bf16[1,400,1536]{2,1,0:T(8,128)(2,1)S(1)} %copy-done.1, f32[1,4,8,768]{3,2,1,0:T(8,128)S(1)} %get-tuple-element.23.left_ref, f32[1,4,8,768]{3,2,1,0:T(8,128)S(1)} %get-tuple-element.24.right_ref, ...), custom_call_target="tpu_custom_call" | custom-call | flops 39321600 | bytes 1228800 | tf_op jit(solution)/shard_map/grid/pallas_call | solution.py:486
  38.8 9.2 %all_to_all.16.back_ref = bf16[32,1,4,192]{3,2,1,0:T(4,128)(2,1)S(1)} all-to-all(bf16[32,1,4,192]{3,2,1,0:T(4,128)(2,1)S(1)} %grid.1), channel_id=1, replica_groups=mesh['lat'=8,'wave'=4] {'lat','wave'}, dimensions={0} | all-to-all | bytes 98304 | tf_op jit(solution)/shard_map/all_to_all | solution.py:495
  48.0 1.7 %backward.1 = f32[8,192,96]{2,1,0:T(8,128)} custom-call(s32[1]{0:T(128)} %bitcast.rank_ref, bf16[32,1,4,192]{3,2,1,0:T(4,128)(2,1)S(1)} %all_to_all.16.back_ref, s32[1,192]{1,0:T(1,128)S(1)} %bitcast.9, bf16[8,96,384]{2,1,0:T(8,128)(2,1)S(1)} %all-to-all-done.legendre_ref.refs_0_), custom_call_target="tpu_custom_call" | custom-call | flops 4718592 | bytes 1179648 | tf_op jit(solution)/shard_map/backward/pallas_call | solution.py:498
  (1 shorter events, 0.0 us)
Async XLA Ops:
  0.0 8.6 %copy-start.6 = (s32[768]{0:T(1024)S(1)}, s32[768]{0:T(1024)}, u32[]{:S(2)}) copy-start(s32[768]{0:T(1024)} %param.8) | copy-start | bytes 9220
  0.0 8.7 %copy-start.2 = (bf16[3,2,2,192,96]{4,3,2,1,0:T(8,128)(2,1)S(1)}, bf16[3,2,2,192,96]{4,3,2,1,0:T(8,128)(2,1)}, u32[]{:S(2)}) copy-start(bf16[3,2,2,192,96]{4,3,2,1,0:T(8,128)(2,1)} %param.6) | copy-start | bytes 1327108
  2.0 7.1 %copy-start.3 = (s32[2]{0:T(128)S(1)}, s32[2]{0:T(128)}, u32[]{:S(2)}) copy-start(s32[2]{0:T(128)} %nlon_ref.1) | copy-start | bytes 28
  2.1 7.1 %copy-start.4 = (f32[2]{0:T(128)S(1)}, f32[2]{0:T(128)}, u32[]{:S(2)}) copy-start(f32[2]{0:T(128)} %coriolis_ref.1) | copy-start | bytes 28
  2.1 7.1 %copy-start.5 = (f32[2]{0:T(128)S(1)}, f32[2]{0:T(128)}, u32[]{:S(2)}) copy-start(f32[2]{0:T(128)} %weight_ref.1) | copy-start | bytes 28
  2.1 23.2 %all-to-all-start = ((bf16[8,96,384]{2,1,0:T(8,128)(2,1)}), bf16[8,96,384]{2,1,0:T(8,128)(2,1)S(1)}, u32[]{:S(2)}, u32[]{:S(2)}) async-start(bf16[8,96,384]{2,1,0:T(8,128)(2,1)} %bitcast.10), calls=%async_computation | async-start | bytes 1179648 | tf_op jit(solution)/shard_map/all_to_all | solution.py:432
  10.3 1.0 %copy-start = (bf16[1,400,1536]{2,1,0:T(8,128)(2,1)}, bf16[1,400,1536]{2,1,0:T(8,128)(2,1)S(1)}, u32[]{:S(2)}) copy-start(bf16[1,400,1536]{2,1,0:T(8,128)(2,1)S(1)} %get-tuple-element.22.table_ref) | copy-start | bytes 3686404
  25.3 12.5 %copy-start.1 = (bf16[1,400,1536]{2,1,0:T(8,128)(2,1)S(1)}, bf16[1,400,1536]{2,1,0:T(8,128)(2,1)}, u32[]{:S(2)}) copy-start(bf16[1,400,1536]{2,1,0:T(8,128)(2,1)} %copy-done) | copy-start | bytes 3686404
